TPU v7x, 128 devices: a whole 4x4x4 slice. The times are simulated.
128 devices in a mesh: blk: 2 (over core), dp: 64 (over z, y, x).
Axes of the slice: x: 4, y: 4, z: 4, core: 2. Of those that a mesh axis runs over, the one named last changes fastest.
Arguments:
- queries: bfloat16 [16384, 256], P(('blk', 'dp')), may hold values from -1 to 1, as said below
- items: bfloat16 [16384, 256], P(('blk', 'dp')), may hold values from -1 to 1, as said below
Outputs:
- loss: float32 [], replicated
- question_slope: float32 [16384, 256], P(('blk', 'dp'))
- candidate_slope: float32 [16384, 256], P(('blk', 'dp'))
Inputs may be any that keep to these rules, and one draw needn't show every extreme that they name: queries: entries lie between -1 and 1 and no row is zero; each query is close to its own item and to one item of the batch chosen by a random permutation (which may be its own). items: entries lie between -1 and 1 and no row is zero.
All inputs are finite; a program needn't handle non-finite values.
Results may differ from a plain program's by a relative error of at most 0.008.
Values may be sent and summed in bfloat16 or wider, within the bound.
A program may use at most 64 MiB of HBM per device.

v0:
```python
import functools
import math

import jax
import jax.numpy as jnp
from jax import lax
from jax.sharding import Mesh
from jax.sharding import PartitionSpec as P

BLK_DP = ("blk", "dp_0", "dp_1", "dp_2")


softmax_sharpness = 0.05
tiny_square = 1e-12


def taken_in(shard, axis, dim, absorb, state):
    everything = jax.tree.map(lambda a: lax.all_gather(a, axis, axis=dim, tiled=True), shard)
    return absorb(state, everything, jnp.int32(0))


def over_axes(value, axes):
    return functools.reduce(lax.psum, axes, value)


def unit_rows(matrix):
    widened = matrix.astype(jnp.float32)
    length = jnp.sqrt(jnp.sum(widened * widened, axis=1, keepdims=True) + tiny_square)
    return (widened / length, length)


def direction_slope(grad, unit, length):
    along = jnp.sum(unit * grad, axis=1, keepdims=True)
    return (grad - unit * along) / length


def split_rows(matrix, step_rows):
    return matrix.reshape((matrix.shape[0] // step_rows, step_rows) + matrix.shape[1:])


def per_device(queries, items):
    question_direction, question_magnitude = unit_rows(queries)
    candidate_direction, candidate_magnitude = unit_rows(items)
    normalized_question = question_direction.astype(jnp.bfloat16)
    normalized_candidate = candidate_direction.astype(jnp.bfloat16)
    question_gathered_all = normalized_question.astype(jnp.float32)
    candidate_gathered_all = normalized_candidate.astype(jnp.float32)
    own_rows = normalized_question.shape[0]
    matching_score = (
        jnp.sum(question_gathered_all * candidate_gathered_all, axis=1) / softmax_sharpness
    )

    def norm_step(running, shard_rows, first_row):
        step_rows = math.gcd(shard_rows.shape[0], 512)

        def per_block(state, candidate_slice):
            old_peak, old_total = state
            similarity_scores = (
                jnp.dot(normalized_question, candidate_slice.T, preferred_element_type=jnp.float32)
                / softmax_sharpness
            )
            new_peak = jnp.maximum(old_peak, jnp.max(similarity_scores, axis=1))
            new_total = old_total * jnp.exp(old_peak - new_peak) + jnp.sum(
                jnp.exp(similarity_scores - new_peak[:, None]), axis=1
            )
            return ((new_peak, new_total), None)

        result, _ = lax.scan(per_block, running, split_rows(shard_rows, step_rows))
        return result

    start_state = (jnp.full((own_rows,), -1e30, jnp.float32), jnp.zeros((own_rows,), jnp.float32))
    peak, summed = taken_in(normalized_candidate, BLK_DP, 0, norm_step, start_state)
    log_norm = peak + jnp.log(summed)
    local_loss = jnp.sum(log_norm - matching_score)
    devices = lax.axis_size(BLK_DP)
    loss = over_axes(local_loss, BLK_DP) / (own_rows * devices)
    empty_grad = jnp.zeros(normalized_question.shape, jnp.float32)

    def query_step(running, shard_rows, first_row):
        step_rows = math.gcd(shard_rows.shape[0], 512)

        def per_block(acc_grad, candidate_slice):
            similarity_scores = (
                jnp.dot(normalized_question, candidate_slice.T, preferred_element_type=jnp.float32)
                / softmax_sharpness
            )
            weights = jnp.exp(similarity_scores - log_norm[:, None]).astype(jnp.bfloat16)
            return (
                acc_grad + jnp.dot(weights, candidate_slice, preferred_element_type=jnp.float32),
                None,
            )

        result, _ = lax.scan(per_block, running, split_rows(shard_rows, step_rows))
        return result

    question_count_overall = taken_in(normalized_candidate, BLK_DP, 0, query_step, empty_grad)

    def item_step(running, shard_rows, first_row):
        q_rows, q_norms = shard_rows
        step_rows = math.gcd(q_rows.shape[0], 512)

        def per_block(acc_grad, pieces):
            question_portion, norm_part = pieces
            question_slice_local = question_portion.astype(jnp.bfloat16)
            similarity_scores = (
                jnp.dot(
                    question_slice_local, normalized_candidate.T, preferred_element_type=jnp.float32
                )
                / softmax_sharpness
            )
            weights = jnp.exp(similarity_scores - norm_part[:, None]).astype(jnp.bfloat16)
            return (
                acc_grad
                + jnp.dot(weights.T, question_slice_local, preferred_element_type=jnp.float32),
                None,
            )

        result, _ = lax.scan(
            per_block, running, (split_rows(q_rows, step_rows), split_rows(q_norms, step_rows))
        )
        return result

    candidate_count_overall = taken_in(
        (question_gathered_all, log_norm), BLK_DP, 0, item_step, empty_grad
    )
    question_slope = direction_slope(
        (question_count_overall - candidate_gathered_all) / softmax_sharpness,
        question_direction,
        question_magnitude,
    )
    candidate_slope = direction_slope(
        (candidate_count_overall - question_gathered_all) / softmax_sharpness,
        candidate_direction,
        candidate_magnitude,
    )
    return (loss, question_slope, candidate_slope)


def solution(mesh):
    split = Mesh(mesh.devices.reshape(mesh.shape["blk"], 4, 4, 4), ("blk", "dp_0", "dp_1", "dp_2"))
    return jax.shard_map(
        per_device,
        mesh=split,
        in_specs=(P(BLK_DP, None), P(BLK_DP, None)),
        out_specs=(P(), P(BLK_DP, None), P(BLK_DP, None)),
        check_vma=False,
    )
```

profile of v0, /device:TPU:1, one launch (start us, length us, event | category | flops | bytes accessed | tf_op | source)
XLA Modules:
  0.0 578.1 jit_solution(8274456256658182323)
XLA Ops:
  8.2 1.6 fusion.37
  10.8 1.6 fusion.38
  12.4 72.5 %all-gather.4.cloned.1.call-done = bf16[16384,256]{1,0:T(8,128)(2,1)} async-done(((bf16[128,256]{1,0:T(8,128)(2,1)}), bf16[16384,256]{1,0:T(8,128)(2,1)}) %all-gather.4.cloned.1.call-update) | async-done | bytes 8388624 | tf_op jit(solution)/shard_map/all_gather | solution.py:18
  84.9 43.2 %while.35 = (s32[]{:T(128)}, f32[128]{0:T(128)S(1)}, f32[128]{0:T(128)S(1)}, bf16[32,512,256]{2,1,0:T(8,128)(2,1)}, bf16[128,256]{1,0:T(8,128)(2,1)}, /*index=5*/s32[]{:T(128)}, s32[]{:T(128)}) while((s32[]{:T(128)}, f32[128]{0:T(128)S(1)}, f32[128]{0:T(128)S(1)}, bf16[32,512,256]{2,1,0:T(8,128)(2,1)}, bf16[128,256]{1,0:T(8,128)(2,1)}, ...), condition=%wide.region_5.0_spmd.clone, body=%wide.region_2.5_spmd.clone.sunk | while | flops 33817216 | bytes 859224 | solution.py:68
  128.1 314.3 %all-gather = f32[128,1,128]{2,1,0:T(1,128)S(1)} all-gather(f32[1,1,128]{2,1,0:T(1,128)S(1)} %bitcast.41), channel_id=1, replica_groups=mesh['blk'=2,'dp_0'=4,'dp_1'=4,'dp_2'=4] {'blk','dp_0','dp_1','dp_2'}, dimensions={0}, use_global_device_ids=true | all-gather | bytes 66048 | tf_op jit(solution)/shard_map/all_gather | solution.py:18
  443.9 50.5 %while.36 = (s32[]{:T(128)}, f32[128,256]{1,0:T(8,128)S(1)}, bf16[32,512,256]{2,1,0:T(8,128)(2,1)}, bf16[128,256]{1,0:T(8,128)(2,1)}, f32[128]{0:T(128)S(1)}, /*index=5*/s32[]{:T(128)}, s32[]{:T(128)}) while((s32[]{:T(128)}, f32[128,256]{1,0:T(8,128)S(1)}, bf16[32,512,256]{2,1,0:T(8,128)(2,1)}, bf16[128,256]{1,0:T(8,128)(2,1)}, ...), condition=%wide.region_13.14_spmd.clone, body=%wide.region_12.13_spmd.clone.sunk | while | flops 67371008 | bytes 853591 | solution.py:93
  443.9 1.6 fusion.62
  445.4 1.6 fusion.62
  447.0 1.6 fusion.62
  448.6 1.6 fusion.62
  450.2 1.6 fusion.62
  451.8 1.6 fusion.62
  453.3 1.6 fusion.62
  454.9 1.6 fusion.62
  456.5 1.6 fusion.62
  458.1 1.6 fusion.62
  459.7 1.6 fusion.62
  461.2 1.6 fusion.62
  462.8 1.6 fusion.62
  464.4 1.6 fusion.62
  466.0 1.6 fusion.62
  467.5 1.6 fusion.62
  469.1 1.6 fusion.62
  470.7 1.6 fusion.62
  472.3 1.6 fusion.62
  473.8 1.6 fusion.62
  475.5 1.6 fusion.62
  477.1 1.6 fusion.62
  478.6 1.6 fusion.62
  480.2 1.6 fusion.62
  481.8 1.6 fusion.62
  483.4 1.6 fusion.62
  484.9 1.6 fusion.62
  486.5 1.6 fusion.62
  488.1 1.6 fusion.62
  489.7 1.6 fusion.62
  491.2 1.6 fusion.62
  492.8 1.6 fusion.62
  494.4 50.1 %while.37 = (s32[]{:T(128)}, f32[128,256]{1,0:T(8,128)S(1)}, bf16[32,512,256]{2,1,0:T(8,128)(2,1)}, bf16[128,256]{1,0:T(8,128)(2,1)S(1)}, f32[32,512]{1,0:T(8,128)S(1)}, /*index=5*/s32[]{:T(128)}, s32[]{:T(128)}) while((s32[]{:T(128)}, f32[128,256]{1,0:T(8,128)S(1)}, bf16[32,512,256]{2,1,0:T(8,128)(2,1)}, ...), condition=%wide.region_16.17_spmd.clone, body=%wide.region_15.16_spmd.clone.sunk | while | flops 67371008 | bytes 859227 | solution.py:118
  494.5 1.5 fusion.66
  496.0 1.5 fusion.66
  497.6 1.5 fusion.66
  499.2 1.5 fusion.66
  503.8 1.5 fusion.66
  505.4 1.5 fusion.66
  507.0 1.5 fusion.66
  511.7 1.5 fusion.66
  513.2 1.5 fusion.66
  514.8 1.5 fusion.66
  519.5 1.5 fusion.66
  521.1 1.5 fusion.66
  522.6 1.5 fusion.66
  525.8 1.6 fusion.66
  527.4 1.5 fusion.66
  528.9 1.5 fusion.66
  530.5 1.5 fusion.66
  532.1 1.5 fusion.66
  536.8 1.5 fusion.66
  538.3 1.5 fusion.66
  539.9 1.5 fusion.66
  545.4 3.1 psum.28
  548.5 6.6 %psum.29 = f32[]{:T(128)} all-reduce(f32[]{:T(128)} %psum.28), channel_id=1, replica_groups=mesh['blk'=2,'dp_0'=4,'dp_1'=4,'dp_2'=4] {'dp_0'}, use_global_device_ids=true, to_apply=%region_9.10 | all-reduce | flops 1 | bytes 8 | tf_op jit(solution)/shard_map/psum | solution.py:23
  555.1 6.6 %psum.30 = f32[]{:T(128)} all-reduce(f32[]{:T(128)} %psum.29), channel_id=1, replica_groups=mesh['blk'=2,'dp_0'=4,'dp_1'=4,'dp_2'=4] {'dp_1'}, use_global_device_ids=true, to_apply=%region_10.11 | all-reduce | flops 1 | bytes 8 | tf_op jit(solution)/shard_map/psum | solution.py:23
  561.7 7.0 %psum.31 = f32[]{:T(128)} all-reduce(f32[]{:T(128)} %psum.30), channel_id=1, replica_groups=mesh['blk'=2,'dp_0'=4,'dp_1'=4,'dp_2'=4] {'dp_2'}, use_global_device_ids=true, to_apply=%region_11.12 | all-reduce | flops 1 | bytes 8 | tf_op jit(solution)/shard_map/psum | solution.py:23
  (229 shorter events, 64.5 us)
Async XLA Ops:
  7.2 537.4 %copy-start.1 = (bf16[128,256]{1,0:T(8,128)(2,1)S(1)}, bf16[128,256]{1,0:T(8,128)(2,1)}, u32[]{:S(2)}) copy-start(bf16[128,256]{1,0:T(8,128)(2,1)} %param.9) | copy-start | bytes 196612
  7.2 537.4 %copy-start.2 = (bf16[128,256]{1,0:T(8,128)(2,1)S(1)}, bf16[128,256]{1,0:T(8,128)(2,1)}, u32[]{:S(2)}) copy-start(bf16[128,256]{1,0:T(8,128)(2,1)} %param.8) | copy-start | bytes 196612
  7.2 77.7 %all-gather.4.cloned.1.call-start = ((), (), s32[]{:S(2)}) async-start(), calls=%async_computation | async-start | bytes 8454144 | tf_op jit(solution)/shard_map/all_gather | solution.py:18
  9.8 484.6 %copy-start = (bf16[128,256]{1,0:T(8,128)(2,1)S(1)}, bf16[128,256]{1,0:T(8,128)(2,1)}, u32[]{:S(2)}) copy-start(bf16[128,256]{1,0:T(8,128)(2,1)} %fusion.37) | copy-start | bytes 196612
  9.8 484.6 %all-gather.6.cloned.1.call-start = ((), (), s32[]{:S(2)}) async-start(), calls=%async_computation.1 | async-start | bytes 8454144 | tf_op jit(solution)/shard_map/all_gather | solution.py:18
Sparse Core Ops, SparseCore 0:
  11.7 73.1 all-gather.3
  88.6 67.3 all-gather.5
where the time goes:
time: 586 us; the launch traced here: 578 us
  blocking collectives  338 us (58%)
  matrix products  137 us (23%)
  waiting for transfers between devices  72.5 us (12%)
  between operations  16 us (3%)
  other arithmetic  11.2 us (2%)
    all_gather x1, blocking collectives, taken_in(): lax.all_gather(a, axis, axis=dim, tiled=True)  314 us
    all_gather x2, waiting for transfers between devices, taken_in(): lax.all_gather(a, axis, axis=dim, tiled=True)  72.5 us
    dot_general x32, matrix products, per_block(): jnp.dot(weights, candidate_slice, preferred_element_type=jnp.float32)  49.8 us
    dot_general x32, matrix products, per_block(): jnp.dot(weights.T, question_slice_local, preferred_element_type=jnp.float32)  48.7 us
    dot_general x32, matrix products, per_block(): jnp.dot(normalized_question, candidate_slice.T, preferred_element_type=jn...  38.6 us
    psum x4, blocking collectives, over_axes(): return functools.reduce(lax.psum, axes, value)  23.3 us
  transfers between devices with their start and end apart: 2, of which 1 were waited for; matrix products, arithmetic and copies ran while one was open for 17% of the time, Pallas kernels for 0%

commit v1 on v0

v1 whole, which is shorter than its diff:
```python
import functools

import jax
import jax.numpy as jnp
from jax import lax
from jax.experimental import pallas as pl
from jax.experimental.pallas import tpu as pltpu
from jax.sharding import PartitionSpec as P

MESH = pl.DeviceIdType.MESH
ROWS = 128
D = 256
BATCH = 16384
INV_TEMP = 20.0
TINY = 1e-12
F32 = jnp.float32
BF16 = jnp.bfloat16
ORDER = (7, 3, 5, 6, 1, 2, 4)


def flip_low(p, d):
    return p + 1 - 2 * (p % 2) if d else p


def flip_high(p, d):
    return 3 - p if d else p


def low_bit(p):
    return ((p + 1) // 2) % 2


def high_bit(p):
    return p // 2


def kernel(
    q_hbm,
    v_hbm,
    loss_ref,
    qs_ref,
    cs_ref,
    q_in,
    v_in,
    q_unit,
    v_unit,
    lens,
    qbuf,
    vbuf,
    t_ref,
    sbuf,
    ub,
    ud,
    us,
    ur,
    qsc,
    wb,
    w_own,
    wr,
    xbuf,
    ybuf,
    in_sem,
    q_send,
    q_recv,
    f_send,
    f_recv,
    v_send,
    v_recv,
    s_send,
    s_recv,
    d_sem,
    u_send,
    u_recv,
    w_send,
    w_recv,
    x_send,
    x_recv,
    y_send,
    y_recv,
):
    core = lax.axis_index("blk")
    other = 1 - core
    dp = lax.axis_index("dp")
    z, y, x = dp // 16, (dp // 4) % 4, dp % 4

    def chip_a(k):
        zz = flip_low(z, (k >> 2) & 1)
        yy = flip_low(y, (k >> 1) & 1)
        xx = flip_low(x, k & 1)
        return zz * 16 + yy * 4 + xx, low_bit(zz) * 4 + low_bit(yy) * 2 + low_bit(xx)

    def chip_b(k):
        zz = flip_high(z, (k >> 2) & 1)
        yy = flip_high(y, (k >> 1) & 1)
        xx = flip_high(x, k & 1)
        return zz * 16 + yy * 4 + xx

    a_chip = [chip_a(k) for k in range(8)]
    b_chip = [chip_b(k) for k in range(8)]
    c_me = a_chip[0][1]
    b_me = high_bit(z) * 4 + high_bit(y) * 2 + high_bit(x)
    lo = pl.multiple_of(core * ROWS, ROWS)

    copies = []

    def send(src, dst, ssem, rsem, blk, chip):
        copy = pltpu.make_async_remote_copy(
            src_ref=src, dst_ref=dst, send_sem=ssem, recv_sem=rsem, device_id=(blk, chip), device_id_type=MESH
        )
        copy.start()
        copies.append(copy)
        return copy

    barrier = pltpu.get_barrier_semaphore()
    for k in ORDER:
        for blk in (core, other):
            pl.semaphore_signal(barrier, inc=1, device_id=(blk, a_chip[k][0]), device_id_type=MESH)
        pl.semaphore_signal(barrier, inc=1, device_id=(core, b_chip[k]), device_id_type=MESH)
    pl.semaphore_signal(barrier, inc=1, device_id=(other, dp), device_id_type=MESH)

    load_q = pltpu.make_async_copy(q_hbm, q_in, in_sem.at[0])
    load_v = pltpu.make_async_copy(v_hbm, v_in, in_sem.at[1])
    load_q.start()
    load_v.start()
    load_q.wait()
    load_v.wait()

    def unit_rows(value):
        wide = value.astype(F32)
        length = jnp.sqrt(jnp.sum(wide * wide, axis=1, keepdims=True) + TINY)
        return wide / length, length

    qu, ql = unit_rows(q_in[...])
    vu, vl = unit_rows(v_in[...])
    q_hat, v_hat = qu.astype(BF16), vu.astype(BF16)
    q_unit[...] = qu
    v_unit[...] = vu
    lens[0] = ql
    lens[1] = vl
    q_own = qbuf.at[c_me, pl.ds(lo, ROWS)]
    qbuf[c_me, pl.ds(lo, ROWS), :] = q_hat
    vbuf[0] = v_hat
    hits = jnp.sum(q_hat.astype(F32) * v_hat.astype(F32), axis=0, keepdims=True)
    positive = (hits[:, :ROWS] + hits[:, ROWS:]) * INV_TEMP

    pl.semaphore_wait(barrier, 22)

    send(q_own, q_own, f_send.at[0], f_recv.at[0], other, dp)
    q_in_flight, v_in_flight = {}, {}
    for k in ORDER:
        q_in_flight[k] = send(q_own, q_own, q_send.at[k], q_recv.at[k], core, a_chip[k][0])
        v_in_flight[k] = send(vbuf.at[0], vbuf.at[k], v_send.at[k], v_recv.at[k], core, b_chip[k])

    for k in (1, 2, 4, 3, 5, 6, 7):
        theirs = qbuf.at[a_chip[k][1], pl.ds(lo, ROWS)]
        q_in_flight[k].wait_recv()
        send(theirs, theirs, f_send.at[k], f_recv.at[k], other, dp)
    for k in ORDER:
        v_in_flight[k].wait_recv()

    def wait_forward(k):
        theirs = qbuf.at[a_chip[k][1], pl.ds(lo, ROWS)]
        pltpu.make_async_remote_copy(
            src_ref=theirs,
            dst_ref=theirs,
            send_sem=f_send.at[k],
            recv_sem=f_recv.at[k],
            device_id=(other, dp),
            device_id_type=MESH,
        ).wait_recv()

    for k in range(8):
        wait_forward(k)

    v_all = vbuf[...].reshape(8 * ROWS, D)
    a_me = core * 8 + c_me
    for c in range(8):
        logits = lax.dot_general(v_all, qbuf[c], (((1,), (1,)), ((), ())), preferred_element_type=F32)
        e = jnp.exp(logits * INV_TEMP)
        sbuf[a_me, pl.ds(c, 1), :] = jnp.sum(e, axis=0, keepdims=True)
        t_ref[c] = e.astype(BF16)

    s_own = sbuf.at[a_me]
    s_copies = [send(s_own, s_own, s_send.at[0], s_recv.at[0], other, dp)]
    for k in ORDER:
        for i, blk in enumerate((core, other)):
            s_copies.append(send(s_own, s_own, s_send.at[2 * k + i], s_recv.at[2 * k + i], blk, a_chip[k][0]))

    for c in range(8):
        ut = lax.dot_general(v_all, t_ref[c], (((0,), (0,)), ((), ())), preferred_element_type=F32)
        ub[0, c] = ut[:, :ROWS].astype(BF16)
        ub[1, c] = ut[:, ROWS:].astype(BF16)
    across = send(ub.at[other], ud, d_sem.at[0], d_sem.at[1], other, dp)

    for copy in s_copies:
        copy.wait_recv()
    total = sbuf[0]
    for a in range(1, 16):
        total = total + sbuf[a]
    inverse = jnp.transpose(1.0 / total)
    for c in range(8):
        qsc[c] = (qbuf[c].astype(F32) * inverse[:, c : c + 1]).astype(BF16)

    w_copies = []
    for half in (1, 0):
        acc = jnp.zeros((4 * ROWS, D), F32)
        for c in range(8):
            acc = acc + jnp.dot(t_ref[c, half * 512 : half * 512 + 512, :], qsc[c], preferred_element_type=F32)
        for j in (3, 2, 1, 0):
            k = half * 4 + j
            part = acc[j * ROWS : (j + 1) * ROWS]
            if k == 0:
                w_own[...] = part
            else:
                wb[k] = part.astype(BF16)
                w_copies.append(send(wb.at[k], wr.at[k], w_send.at[k], w_recv.at[k], core, b_chip[k]))

    mine = lax.broadcasted_iota(jnp.int32, total.shape, 0) == c_me
    s_row = jnp.sum(jnp.where(mine, total, 0.0), axis=0, keepdims=True)
    s_row = jnp.where(core == 0, s_row[:, :ROWS], s_row[:, ROWS:])
    xbuf[b_me] = jnp.zeros((8, ROWS), F32)
    xbuf[b_me, 0:1, :] = jnp.log(s_row) - positive
    x_copies = [
        send(xbuf.at[b_me], xbuf.at[b_me], x_send.at[k], x_recv.at[k], core, b_chip[k]) for k in ORDER
    ]

    across.wait_recv()
    for c in range(8):
        us[c] = (ub[core, c].astype(F32) + ud[c].astype(F32)).astype(BF16)
    u_copies = [
        send(us.at[a_chip[k][1]], ur.at[k], u_send.at[k], u_recv.at[k], core, a_chip[k][0]) for k in ORDER
    ]

    for copy in x_copies:
        copy.wait_recv()
    x_sum = xbuf[0]
    for b in range(1, 8):
        x_sum = x_sum + xbuf[b]
    ybuf[a_me] = x_sum
    y_copies = [send(ybuf.at[a_me], ybuf.at[a_me], y_send.at[0], y_recv.at[0], other, dp)]
    for k in ORDER:
        for i, blk in enumerate((core, other)):
            y_copies.append(
                send(ybuf.at[a_me], ybuf.at[a_me], y_send.at[2 * k + i], y_recv.at[2 * k + i], blk, a_chip[k][0])
            )

    def slope(pull, unit, length):
        along = jnp.sum(unit * pull, axis=1, keepdims=True)
        return (pull - unit * along) / length

    for copy in u_copies:
        copy.wait_recv()
    u_sum = ub[core, c_me].astype(F32) + ud[c_me].astype(F32)
    for k in range(1, 8):
        u_sum = u_sum + ur[k].astype(F32)
    q_pull = (jnp.transpose(u_sum / s_row) - vbuf[0].astype(F32)) * INV_TEMP
    qs_ref[...] = slope(q_pull, q_unit[...], lens[0])

    for copy in w_copies:
        copy.wait_recv()
    w_sum = w_own[...]
    for k in range(1, 8):
        w_sum = w_sum + wr[k].astype(F32)
    v_pull = (w_sum - qbuf[c_me, pl.ds(lo, ROWS), :].astype(F32)) * INV_TEMP
    cs_ref[...] = slope(v_pull, v_unit[...], lens[1])

    for copy in y_copies:
        copy.wait_recv()
    y_sum = ybuf[0]
    for a in range(1, 16):
        y_sum = y_sum + ybuf[a]
    loss_ref[0, 0] = jnp.sum(y_sum) / BATCH

    for copy in copies:
        copy.wait_send()


def per_device(queries, items):
    dma = pltpu.SemaphoreType.DMA
    vmem = pltpu.VMEM
    loss, q_slope, v_slope = pl.pallas_call(
        kernel,
        out_shape=(
            jax.ShapeDtypeStruct((1, 1), F32),
            jax.ShapeDtypeStruct((ROWS, D), F32),
            jax.ShapeDtypeStruct((ROWS, D), F32),
        ),
        in_specs=[pl.BlockSpec(memory_space=pl.ANY)] * 2,
        out_specs=(
            pl.BlockSpec(memory_space=pltpu.SMEM),
            pl.BlockSpec(memory_space=pltpu.VMEM),
            pl.BlockSpec(memory_space=pltpu.VMEM),
        ),
        scratch_shapes=[
            vmem((ROWS, D), BF16),
            vmem((ROWS, D), BF16),
            vmem((ROWS, D), F32),
            vmem((ROWS, D), F32),
            vmem((2, ROWS, 1), F32),
            vmem((8, 2 * ROWS, D), BF16),
            vmem((8, ROWS, D), BF16),
            vmem((8, 8 * ROWS, 2 * ROWS), BF16),
            vmem((16, 8, 2 * ROWS), F32),
            vmem((2, 8, D, ROWS), BF16),
            vmem((8, D, ROWS), BF16),
            vmem((8, D, ROWS), BF16),
            vmem((8, D, ROWS), BF16),
            vmem((8, 2 * ROWS, D), BF16),
            vmem((8, ROWS, D), BF16),
            vmem((ROWS, D), F32),
            vmem((8, ROWS, D), BF16),
            vmem((8, 8, ROWS), F32),
            vmem((16, 8, ROWS), F32),
            dma((2,)),
            dma((8,)),
            dma((8,)),
            dma((8,)),
            dma((8,)),
            dma((8,)),
            dma((8,)),
            dma((16,)),
            dma((16,)),
            dma((2,)),
            dma((8,)),
            dma((8,)),
            dma((8,)),
            dma((8,)),
            dma((8,)),
            dma((8,)),
            dma((16,)),
            dma((16,)),
        ],
        compiler_params=pltpu.CompilerParams(collective_id=0, has_side_effects=True),
    )(queries, items)
    return loss.reshape(()), q_slope, v_slope


def solution(mesh):
    spec = P(("blk", "dp"), None)
    return jax.shard_map(
        per_device, mesh=mesh, in_specs=(spec, spec), out_specs=(P(), spec, spec), check_vma=False
    )
```

time: 586 us -> 44.3 us (0.08); the launches traced: 578 us -> 44.1 us
  blocking collectives: 338 us -> 0 us
  matrix products: 137 us -> 0 us
  waiting for transfers between devices: 72.5 us -> 0 us
  Pallas kernels: 0 us -> 39.6 us
  between operations: 16 us -> 2.32 us
  other arithmetic: 11.2 us -> 0 us
    all_gather x1 -> x0, blocking collectives: 314 us -> none  [taken_in(): lax.all_gather(a, axis, axis=dim, tiled=True)]
    dot_general x96 -> x0, matrix products: 137 us -> none  [the longest x32 49.8 us: per_block(): jnp.dot(weights, candidate_slice, preferred_element_type=jnp.float32)]
    all_gather x2 -> x0, waiting for transfers between devices: 72.5 us -> none  [taken_in(): lax.all_gather(a, axis, axis=dim, tiled=True)]
    pallas_call x0 -> x1, Pallas kernels: none -> 39.6 us  [per_device(): pl.pallas_call(kernel, out_shape=(jax.ShapeDtypeStruct((1, 1), F32), jax....]
    psum x4 -> x0, blocking collectives: 23.3 us -> none  [over_axes(): return functools.reduce(lax.psum, axes, value)]
  transfers between devices with their start and end apart: 2 -> 0, of which waited for: 1 -> 0; matrix products, arithmetic and copies ran while one was open for 17% -> 0% of each run, Pallas kernels for 0% -> 0%
where the time goes in v1:
time: 44.3 us; the launch traced here: 44.1 us
  Pallas kernels  39.6 us (89%)
  between operations  2.32 us (5%)
  local copies, waits for them, and re-layouts  2.26 us (5%)
    pallas_call x1, Pallas kernels, per_device(): pl.pallas_call(kernel, out_shape=(jax.ShapeDtypeStruct((1, 1), F32), jax....  39.6 us
    unnamed x4, local copies, waits for them, and re-layouts  2.26 us

profile of v1, /device:TPU:1, one launch (start us, length us, event | category | flops | bytes accessed | tf_op | source)
XLA Modules:
  0.0 44.1 jit_solution(8615159453865584269)
XLA Ops:
  0.6 39.6 %shard_map.49 = (f32[1,1]{1,0:T(1,128)}, f32[128,256]{1,0:T(8,128)}, f32[128,256]{1,0:T(8,128)}) custom-call(bf16[128,256]{1,0:T(8,128)(2,1)} %q_hbm.1, bf16[128,256]{1,0:T(8,128)(2,1)} %v_hbm.1), custom_call_target="tpu_custom_call" | custom-call | tf_op jit(solution)/shard_map/pallas_call | solution.py:281
  40.7 0.0 copy-start
  40.7 1.6 %copy.9 = f32[128,256]{1,0:T(8,128)} copy(f32[128,256]{1,0:T(8,128)} %get-tuple-element.13) | data formatting | bytes 262144
  42.3 0.0 copy-done
  42.4 0.7 %copy.10 = f32[128,256]{1,0:T(8,128)} copy(f32[128,256]{1,0:T(8,128)S(1)} %copy-done) | data formatting | bytes 262144
Async XLA Ops:
  40.7 1.6 %copy-start = (f32[128,256]{1,0:T(8,128)S(1)}, f32[128,256]{1,0:T(8,128)}, u32[]{:S(2)}) copy-start(f32[128,256]{1,0:T(8,128)} %get-tuple-element.14) | copy-start | bytes 393220

commit v2 on v1

v2 whole, which is shorter than its diff:
```python
import functools

import jax
import jax.numpy as jnp
from jax import lax
from jax.experimental import pallas as pl
from jax.experimental.pallas import tpu as pltpu
from jax.sharding import PartitionSpec as P

MESH = pl.DeviceIdType.MESH
ROWS = 128
D = 256
BATCH = 16384
INV_TEMP = 20.0
TINY = 1e-12
F32 = jnp.float32
BF16 = jnp.bfloat16
ORDER = (7, 3, 5, 6, 1, 2, 4)


def flip_low(p, d):
    return p + 1 - 2 * lax.rem(p, 2) if d else p


def flip_high(p, d):
    return 3 - p if d else p


def low_bit(p):
    return lax.rem(lax.div(p + 1, 2), 2)


def high_bit(p):
    return lax.div(p, 2)


def kernel(
    q_hbm,
    v_hbm,
    hits_ref,
    qs_ref,
    cs_ref,
    q_in,
    v_in,
    q_unit,
    v_unit,
    lens,
    qbuf,
    vbuf,
    t_ref,
    sbuf,
    ub,
    ud,
    us,
    ur,
    qsc,
    wb,
    w_own,
    wr,
    xbuf,
    ybuf,
    in_sem,
    q_send,
    q_recv,
    f_send,
    f_recv,
    v_send,
    v_recv,
    s_send,
    s_recv,
    d_sem,
    u_send,
    u_recv,
    w_send,
    w_recv,
    x_send,
    x_recv,
    y_send,
    y_recv,
    near_sem,
    far_sem,
):
    core = lax.axis_index("blk")
    other = 1 - core
    dp = lax.axis_index("dp")
    z, y, x = lax.div(dp, 16), lax.rem(lax.div(dp, 4), 4), lax.rem(dp, 4)

    def chip_a(k):
        zz = flip_low(z, (k >> 2) & 1)
        yy = flip_low(y, (k >> 1) & 1)
        xx = flip_low(x, k & 1)
        return zz * 16 + yy * 4 + xx, low_bit(zz) * 4 + low_bit(yy) * 2 + low_bit(xx)

    def chip_b(k):
        zz = flip_high(z, (k >> 2) & 1)
        yy = flip_high(y, (k >> 1) & 1)
        xx = flip_high(x, k & 1)
        return zz * 16 + yy * 4 + xx

    a_chip = [chip_a(k) for k in range(8)]
    b_chip = [chip_b(k) for k in range(8)]
    c_me = a_chip[0][1]
    b_me = high_bit(z) * 4 + high_bit(y) * 2 + high_bit(x)
    lo = pl.multiple_of(core * ROWS, ROWS)

    copies = []

    def send(src, dst, ssem, rsem, blk, chip):
        copy = pltpu.make_async_remote_copy(
            src_ref=src, dst_ref=dst, send_sem=ssem, recv_sem=rsem, device_id=(blk, chip), device_id_type=MESH
        )
        copy.start()
        copies.append(copy)
        return copy

    barrier = pltpu.get_barrier_semaphore()

    def tell(sem, blk, chip):
        pl.semaphore_signal(sem, inc=1, device_id=(blk, chip), device_id_type=MESH)

    for d in range(3):
        tell(barrier, core, a_chip[1 << d][0])
        tell(barrier, core, b_chip[1 << d])
    tell(barrier, other, dp)

    load_q = pltpu.make_async_copy(q_hbm, q_in, in_sem.at[0])
    load_v = pltpu.make_async_copy(v_hbm, v_in, in_sem.at[1])
    load_q.start()
    load_v.start()
    load_q.wait()
    load_v.wait()

    def unit_rows(value):
        wide = value.astype(F32)
        length = jnp.sqrt(jnp.sum(wide * wide, axis=1, keepdims=True) + TINY)
        return wide / length, length

    qu, ql = unit_rows(q_in[...])
    vu, vl = unit_rows(v_in[...])
    q_hat, v_hat = qu.astype(BF16), vu.astype(BF16)
    q_unit[...] = qu
    v_unit[...] = vu
    lens[0] = ql
    lens[1] = vl
    q_own = qbuf.at[c_me, pl.ds(lo, ROWS)]
    qbuf[c_me, pl.ds(lo, ROWS), :] = q_hat
    vbuf[0] = v_hat
    hits = jnp.sum(q_hat.astype(F32) * v_hat.astype(F32), axis=0, keepdims=True)
    ybuf[core * 8 + c_me] = jnp.broadcast_to(hits[:, :ROWS] + hits[:, ROWS:], (8, ROWS))

    pl.semaphore_wait(barrier, 7)
    for d in range(3):
        tell(near_sem.at[d], core, a_chip[1 << d][0])
        tell(near_sem.at[3 + d], core, b_chip[1 << d])

    q_flight, v_flight, f_flight = {}, {}, {}

    def gather(k):
        q_flight[k] = send(q_own, q_own, q_send.at[k], q_recv.at[k], core, a_chip[k][0])
        v_flight[k] = send(vbuf.at[0], vbuf.at[k], v_send.at[k], v_recv.at[k], core, b_chip[k])

    f_flight[0] = send(q_own, q_own, f_send.at[0], f_recv.at[0], other, dp)
    for k in (1, 2, 4):
        gather(k)
    for d in range(6):
        pl.semaphore_wait(near_sem.at[d], 1)
    tell(far_sem.at[0], core, a_chip[1][0])
    tell(far_sem.at[1], core, b_chip[1])
    for k in (3, 5, 6):
        gather(k)
    for d in range(2):
        pl.semaphore_wait(far_sem.at[d], 1)
    gather(7)

    for k in (1, 2, 4, 3, 5, 6, 7):
        theirs = qbuf.at[a_chip[k][1], pl.ds(lo, ROWS)]
        q_flight[k].wait_recv()
        f_flight[k] = send(theirs, theirs, f_send.at[k], f_recv.at[k], other, dp)
    for k in range(1, 8):
        v_flight[k].wait_recv()

    for k in range(8):
        f_flight[k].wait_recv()

    v_all = vbuf[...].reshape(8 * ROWS, D)
    a_me = core * 8 + c_me
    for c in range(8):
        logits = lax.dot_general(v_all, qbuf[c], (((1,), (1,)), ((), ())), preferred_element_type=F32)
        e = jnp.exp(logits * INV_TEMP)
        sbuf[a_me, pl.ds(c, 1), :] = jnp.sum(e, axis=0, keepdims=True)
        t_ref[c] = e.astype(BF16)

    def exchange(ref, ssem, rsem):
        flight = []
        for k in ORDER:
            for i, blk in enumerate((core, other)):
                n = 2 * k + i
                flight.append(send(ref, ref, ssem.at[n], rsem.at[n], blk, a_chip[k][0]))
        flight.append(send(ref, ref, ssem.at[0], rsem.at[0], other, dp))
        return flight

    s_flight = exchange(sbuf.at[a_me], s_send, s_recv)
    y_flight = exchange(ybuf.at[a_me], y_send, y_recv)

    for c in range(8):
        ut = lax.dot_general(v_all, t_ref[c], (((0,), (0,)), ((), ())), preferred_element_type=F32)
        ub[0, c] = ut[:, :ROWS].astype(BF16)
        ub[1, c] = ut[:, ROWS:].astype(BF16)
    across = send(ub.at[other], ud, d_sem.at[0], d_sem.at[1], other, dp)

    across.wait_recv()
    for c in range(8):
        us[c] = (ub[core, c].astype(F32) + ud[c].astype(F32)).astype(BF16)
    u_flight = [
        send(us.at[a_chip[k][1]], ur.at[k], u_send.at[k], u_recv.at[k], core, a_chip[k][0]) for k in ORDER
    ]

    for copy in s_flight:
        copy.wait_recv()
    total = sbuf[0]
    for a in range(1, 16):
        total = total + sbuf[a]
    inverse = jnp.transpose(1.0 / total)
    for c in range(8):
        qsc[c] = (qbuf[c].astype(F32) * inverse[:, c : c + 1]).astype(BF16)

    for copy in y_flight:
        copy.wait_recv()
    hits = ybuf[0]
    for a in range(1, 16):
        hits = hits + ybuf[a]
    logs = jnp.log(total)
    xbuf[b_me] = (logs[:, :ROWS] + logs[:, ROWS:]) - hits * (INV_TEMP / 8.0)
    x_flight = [
        send(xbuf.at[b_me], xbuf.at[b_me], x_send.at[k], x_recv.at[k], core, b_chip[k]) for k in ORDER
    ]

    w_flight = []
    for half in (1, 0):
        acc = jnp.zeros((4 * ROWS, D), F32)
        for c in range(8):
            acc = acc + jnp.dot(t_ref[c, half * 512 : half * 512 + 512, :], qsc[c], preferred_element_type=F32)
        for j in (3, 2, 1, 0):
            k = half * 4 + j
            part = acc[j * ROWS : (j + 1) * ROWS]
            if k == 0:
                w_own[...] = part
            else:
                wb[k] = part.astype(BF16)
                w_flight.append(send(wb.at[k], wr.at[k], w_send.at[k], w_recv.at[k], core, b_chip[k]))

    mine = lax.broadcasted_iota(jnp.int32, total.shape, 0) == c_me
    s_row = jnp.sum(jnp.where(mine, total, 0.0), axis=0, keepdims=True)
    s_row = jnp.where(core == 0, s_row[:, :ROWS], s_row[:, ROWS:])

    def slope(pull, unit, length):
        along = jnp.sum(unit * pull, axis=1, keepdims=True)
        return (pull - unit * along) / length

    for copy in u_flight:
        copy.wait_recv()
    u_sum = ub[core, c_me].astype(F32) + ud[c_me].astype(F32)
    for k in range(1, 8):
        u_sum = u_sum + ur[k].astype(F32)
    q_pull = (jnp.transpose(u_sum / s_row) - vbuf[0].astype(F32)) * INV_TEMP
    qs_ref[...] = slope(q_pull, q_unit[...], lens[0])

    for copy in w_flight:
        copy.wait_recv()
    w_sum = w_own[...]
    for k in range(1, 8):
        w_sum = w_sum + wr[k].astype(F32)
    v_pull = (w_sum - qbuf[c_me, pl.ds(lo, ROWS), :].astype(F32)) * INV_TEMP
    cs_ref[...] = slope(v_pull, v_unit[...], lens[1])

    for copy in x_flight:
        copy.wait_recv()
    x_sum = xbuf[0]
    for b in range(1, 8):
        x_sum = x_sum + xbuf[b]
    hits_ref[...] = x_sum

    for copy in copies:
        copy.wait_send()


def write_out(l_ref, q_ref, v_ref, l_out, q_out, v_out, l_own, sem):
    q_copy = pltpu.make_async_copy(q_ref, q_out, sem.at[0])
    v_copy = pltpu.make_async_copy(v_ref, v_out, sem.at[1])
    q_copy.start()
    v_copy.start()
    l_own[0, 0] = jnp.sum(l_ref[...]) / BATCH
    l_copy = pltpu.make_async_copy(l_own, l_out, sem.at[2])
    l_copy.start()
    l_copy.wait()
    q_copy.wait()
    v_copy.wait()


def per_device(queries, items):
    dma = pltpu.SemaphoreType.DMA
    vmem = pltpu.VMEM
    parts = pl.pallas_call(
        kernel,
        out_shape=(vmem((8, ROWS), F32), vmem((ROWS, D), F32), vmem((ROWS, D), F32)),
        in_specs=[pl.BlockSpec(memory_space=pltpu.HBM)] * 2,
        out_specs=(pl.BlockSpec(memory_space=vmem),) * 3,
        scratch_shapes=[
            vmem((ROWS, D), BF16),
            vmem((ROWS, D), BF16),
            vmem((ROWS, D), F32),
            vmem((ROWS, D), F32),
            vmem((2, ROWS, 1), F32),
            vmem((8, 2 * ROWS, D), BF16),
            vmem((8, ROWS, D), BF16),
            vmem((8, 8 * ROWS, 2 * ROWS), BF16),
            vmem((16, 8, 2 * ROWS), F32),
            vmem((2, 8, D, ROWS), BF16),
            vmem((8, D, ROWS), BF16),
            vmem((8, D, ROWS), BF16),
            vmem((8, D, ROWS), BF16),
            vmem((8, 2 * ROWS, D), BF16),
            vmem((8, ROWS, D), BF16),
            vmem((ROWS, D), F32),
            vmem((8, ROWS, D), BF16),
            vmem((8, 8, ROWS), F32),
            vmem((16, 8, ROWS), F32),
            dma((2,)),
            dma((8,)),
            dma((8,)),
            dma((8,)),
            dma((8,)),
            dma((8,)),
            dma((8,)),
            dma((16,)),
            dma((16,)),
            dma((2,)),
            dma((8,)),
            dma((8,)),
            dma((8,)),
            dma((8,)),
            dma((8,)),
            dma((8,)),
            dma((16,)),
            dma((16,)),
            pltpu.SemaphoreType.REGULAR((6,)),
            pltpu.SemaphoreType.REGULAR((2,)),
        ],
        compiler_params=pltpu.CompilerParams(collective_id=0, has_side_effects=True),
    )(queries, items)
    loss, q_slope, v_slope = pl.pallas_call(
        write_out,
        out_shape=(
            jax.ShapeDtypeStruct((1, 1), F32),
            jax.ShapeDtypeStruct((ROWS, D), F32),
            jax.ShapeDtypeStruct((ROWS, D), F32),
        ),
        in_specs=[pl.BlockSpec(memory_space=vmem)] * 3,
        out_specs=(
            pl.BlockSpec(memory_space=pltpu.HBM),
            pl.BlockSpec(memory_space=pltpu.HBM),
            pl.BlockSpec(memory_space=pltpu.HBM),
        ),
        scratch_shapes=[pltpu.SMEM((1, 1), F32), dma((3,))],
        compiler_params=pltpu.CompilerParams(vmem_limit_bytes=1024 * 1024),
    )(*(pltpu.with_memory_space_constraint(part, vmem) for part in parts))
    return loss.reshape(()), q_slope, v_slope


def solution(mesh):
    spec = P(("blk", "dp"), None)
    return jax.shard_map(
        per_device, mesh=mesh, in_specs=(spec, spec), out_specs=(P(), spec, spec), check_vma=False
    )
```

time: 44.3 us -> 37.2 us (0.84)
  Pallas kernels: 39.6 us -> 36.4 us
  local copies, waits for them, and re-layouts: 2.26 us -> 0 us
  between operations: 2.32 us -> 0.64 us
    pallas_call x1 -> x2, Pallas kernels: 39.6 us -> 36.4 us  [the longest x1 35.6 us: per_device(): pl.pallas_call(kernel, out_shape=(vmem((8, ROWS), F32), vmem((ROWS, D), F...]
    unnamed x4 -> x0, local copies, waits for them, and re-layouts: 2.26 us -> none
where the time goes in v2:
time: 37.2 us; the launch traced here: 37 us
  Pallas kernels  36.4 us (98%)
  between operations  0.64 us (2%)
    pallas_call x1, Pallas kernels, per_device(): pl.pallas_call(kernel, out_shape=(vmem((8, ROWS), F32), vmem((ROWS, D), F...  35.6 us

profile of v2, /device:TPU:1, one launch (start us, length us, event | category | flops | bytes accessed | tf_op | source)
XLA Modules:
  0.0 37.0 jit_solution(12887374330388645402)
XLA Ops:
  0.6 35.6 %shard_map.49 = (f32[8,128]{1,0:T(8,128)S(1)}, f32[128,256]{1,0:T(8,128)S(1)}, f32[128,256]{1,0:T(8,128)S(1)}) custom-call(bf16[128,256]{1,0:T(8,128)(2,1)} %q_hbm.1, bf16[128,256]{1,0:T(8,128)(2,1)} %v_hbm.1), custom_call_target="tpu_custom_call" | custom-call | tf_op jit(solution)/shard_map/pallas_call | solution.py:303
  36.3 0.7 %shard_map.50 = (f32[1,1]{1,0:T(1,128)}, f32[128,256]{1,0:T(8,128)}, f32[128,256]{1,0:T(8,128)}) custom-call(f32[8,128]{1,0:T(8,128)S(1)} %get-tuple-element.9.l_ref, f32[128,256]{1,0:T(8,128)S(1)} %get-tuple-element.10.q_ref, f32[128,256]{1,0:T(8,128)S(1)} %get-tuple-element.11.v_ref), custom_call_target="tpu_custom_call" | custom-call | tf_op jit(solution)/shard_map/pallas_call | solution.py:351

commit v3 on v2

--- a/solution.py
+++ b/solution.py
@@ -1,5 +1,3 @@
-import functools
-
 import jax
 import jax.numpy as jnp
 from jax import lax
@@ -15,6 +13,9 @@
 TINY = 1e-12
 F32 = jnp.float32
 BF16 = jnp.bfloat16
+A_LOW = (True, True, True)
+SLOT = (0, 1, 2, 4, 3, 5, 6, 7)
+NEAR, FAR = (0, 1, 2, 4), (3, 5, 6, 7)
 ORDER = (7, 3, 5, 6, 1, 2, 4)
 
 
@@ -49,6 +50,7 @@
     vbuf,
     t_ref,
     sbuf,
+    spart,
     ub,
     ud,
     us,
@@ -79,36 +81,44 @@
     y_recv,
     near_sem,
     far_sem,
+    side_sem,
 ):
     core = lax.axis_index("blk")
     other = 1 - core
     dp = lax.axis_index("dp")
     z, y, x = lax.div(dp, 16), lax.rem(lax.div(dp, 4), 4), lax.rem(dp, 4)
 
-    def chip_a(k):
-        zz = flip_low(z, (k >> 2) & 1)
-        yy = flip_low(y, (k >> 1) & 1)
-        xx = flip_low(x, k & 1)
-        return zz * 16 + yy * 4 + xx, low_bit(zz) * 4 + low_bit(yy) * 2 + low_bit(xx)
-
-    def chip_b(k):
-        zz = flip_high(z, (k >> 2) & 1)
-        yy = flip_high(y, (k >> 1) & 1)
-        xx = flip_high(x, k & 1)
-        return zz * 16 + yy * 4 + xx
-
-    a_chip = [chip_a(k) for k in range(8)]
-    b_chip = [chip_b(k) for k in range(8)]
+    place = (z, y, x)
+
+    def partner(k, low):
+        steps = ((k >> 2) & 1, (k >> 1) & 1, k & 1)
+        zz, yy, xx = (
+            (flip_low if is_low == low else flip_high)(p, d) for p, d, is_low in zip(place, steps, A_LOW)
+        )
+        return zz, yy, xx
+
+    def rank(place, low):
+        bits = [(low_bit if is_low == low else high_bit)(p) for p, is_low in zip(place, A_LOW)]
+        return bits[0] * 4 + bits[1] * 2 + bits[2]
+
+    def number(place):
+        return place[0] * 16 + place[1] * 4 + place[2]
+
+    a_chip = [(number(partner(k, True)), rank(partner(k, True), True)) for k in range(8)]
+    b_chip = [number(partner(k, False)) for k in range(8)]
     c_me = a_chip[0][1]
-    b_me = high_bit(z) * 4 + high_bit(y) * 2 + high_bit(x)
+    b_me = rank(place, False)
     lo = pl.multiple_of(core * ROWS, ROWS)
 
     copies = []
 
-    def send(src, dst, ssem, rsem, blk, chip):
-        copy = pltpu.make_async_remote_copy(
+    def plan(src, dst, ssem, rsem, blk, chip):
+        return pltpu.make_async_remote_copy(
             src_ref=src, dst_ref=dst, send_sem=ssem, recv_sem=rsem, device_id=(blk, chip), device_id_type=MESH
         )
+
+    def send(*where):
+        copy = plan(*where)
         copy.start()
         copies.append(copy)
         return copy
@@ -146,7 +156,7 @@
     qbuf[c_me, pl.ds(lo, ROWS), :] = q_hat
     vbuf[0] = v_hat
     hits = jnp.sum(q_hat.astype(F32) * v_hat.astype(F32), axis=0, keepdims=True)
-    ybuf[core * 8 + c_me] = jnp.broadcast_to(hits[:, :ROWS] + hits[:, ROWS:], (8, ROWS))
+    ybuf[core * 8 + c_me] = hits[:, :ROWS] + hits[:, ROWS:]
 
     pl.semaphore_wait(barrier, 7)
     for d in range(3):
@@ -155,40 +165,68 @@
 
     q_flight, v_flight, f_flight = {}, {}, {}
 
-    def gather(k):
+    def gather_q(k):
         q_flight[k] = send(q_own, q_own, q_send.at[k], q_recv.at[k], core, a_chip[k][0])
-        v_flight[k] = send(vbuf.at[0], vbuf.at[k], v_send.at[k], v_recv.at[k], core, b_chip[k])
+
+    def gather_v(k):
+        v_flight[k] = send(vbuf.at[0], vbuf.at[SLOT[k]], v_send.at[k], v_recv.at[k], core, b_chip[k])
 
     f_flight[0] = send(q_own, q_own, f_send.at[0], f_recv.at[0], other, dp)
     for k in (1, 2, 4):
-        gather(k)
-    for d in range(6):
+        gather_v(k)
+        gather_q(k)
+    for d in range(3):
         pl.semaphore_wait(near_sem.at[d], 1)
     tell(far_sem.at[0], core, a_chip[1][0])
+    for k in (3, 5, 6):
+        gather_q(k)
+    for d in range(3, 6):
+        pl.semaphore_wait(near_sem.at[d], 1)
     tell(far_sem.at[1], core, b_chip[1])
     for k in (3, 5, 6):
-        gather(k)
-    for d in range(2):
-        pl.semaphore_wait(far_sem.at[d], 1)
-    gather(7)
-
-    for k in (1, 2, 4, 3, 5, 6, 7):
-        theirs = qbuf.at[a_chip[k][1], pl.ds(lo, ROWS)]
-        q_flight[k].wait_recv()
-        f_flight[k] = send(theirs, theirs, f_send.at[k], f_recv.at[k], other, dp)
-    for k in range(1, 8):
+        gather_v(k)
+    pl.semaphore_wait(far_sem.at[0], 1)
+    gather_q(7)
+    pl.semaphore_wait(far_sem.at[1], 1)
+    gather_v(7)
+    tell(side_sem, other, dp)
+    pl.semaphore_wait(side_sem, 1)
+    f_flight[7] = send(q_own, q_own, f_send.at[7], f_recv.at[7], other, a_chip[7][0])
+
+    def pass_on(ks):
+        for k in ks:
+            theirs = qbuf.at[a_chip[k][1], pl.ds(lo, ROWS)]
+            q_flight[k].wait_recv()
+            f_flight[k] = send(theirs, theirs, f_send.at[k], f_recv.at[k], other, dp)
+
+    def weigh(half, ks):
+        rows = slice(half * 512, half * 512 + 512)
+        v_half = vbuf[half * 4 : half * 4 + 4].reshape(512, D)
+        for k in ks:
+            c = a_chip[k][1]
+            logits = lax.dot_general(v_half, qbuf[c], (((1,), (1,)), ((), ())), preferred_element_type=F32)
+            e = jnp.exp(logits * INV_TEMP)
+            spart[half, c, 0:1, :] = jnp.sum(e, axis=0, keepdims=True)
+            t_ref[c, rows, :] = e.astype(BF16)
+
+    pass_on(NEAR[1:])
+    for k in NEAR[1:]:
         v_flight[k].wait_recv()
-
-    for k in range(8):
+    for k in NEAR:
         f_flight[k].wait_recv()
-
-    v_all = vbuf[...].reshape(8 * ROWS, D)
+    weigh(0, NEAR)
+    pass_on(FAR[:3])
+    q_flight[7].wait_recv()
+    for k in FAR:
+        f_flight[k].wait_recv()
+    weigh(0, FAR)
+    for k in FAR:
+        v_flight[k].wait_recv()
+    weigh(1, range(8))
     a_me = core * 8 + c_me
     for c in range(8):
-        logits = lax.dot_general(v_all, qbuf[c], (((1,), (1,)), ((), ())), preferred_element_type=F32)
-        e = jnp.exp(logits * INV_TEMP)
-        sbuf[a_me, pl.ds(c, 1), :] = jnp.sum(e, axis=0, keepdims=True)
-        t_ref[c] = e.astype(BF16)
+        sbuf[a_me, c : c + 1, :] = spart[0, c, 0:1, :] + spart[1, c, 0:1, :]
+    v_all = vbuf[...].reshape(8 * ROWS, D)
 
     def exchange(ref, ssem, rsem):
         flight = []
@@ -224,30 +262,41 @@
     for c in range(8):
         qsc[c] = (qbuf[c].astype(F32) * inverse[:, c : c + 1]).astype(BF16)
 
-    for copy in y_flight:
-        copy.wait_recv()
-    hits = ybuf[0]
-    for a in range(1, 16):
-        hits = hits + ybuf[a]
-    logs = jnp.log(total)
-    xbuf[b_me] = (logs[:, :ROWS] + logs[:, ROWS:]) - hits * (INV_TEMP / 8.0)
-    x_flight = [
-        send(xbuf.at[b_me], xbuf.at[b_me], x_send.at[k], x_recv.at[k], core, b_chip[k]) for k in ORDER
-    ]
-
-    w_flight = []
-    for half in (1, 0):
-        acc = jnp.zeros((4 * ROWS, D), F32)
-        for c in range(8):
-            acc = acc + jnp.dot(t_ref[c, half * 512 : half * 512 + 512, :], qsc[c], preferred_element_type=F32)
-        for j in (3, 2, 1, 0):
-            k = half * 4 + j
+    x_flight = []
+
+    def loss_rows():
+        for copy in y_flight:
+            copy.wait_recv()
+        hits = ybuf[0]
+        for a in range(1, 16):
+            hits = hits + ybuf[a]
+        logs = jnp.sum(jnp.log(total), axis=0, keepdims=True)
+        xbuf[b_me] = (logs[:, :ROWS] + logs[:, ROWS:]) - hits * INV_TEMP
+        for k in ORDER:
+            x_flight.append(send(xbuf.at[b_me], xbuf.at[b_me], x_send.at[k], x_recv.at[k], core, b_chip[k]))
+
+    w_flight = {
+        k: plan(wb.at[k], wr.at[k], w_send.at[k], w_recv.at[k], core, b_chip[k]) for k in range(1, 8)
+    }
+
+    def w_chunk(quarter):
+        rows = slice(quarter * 256, quarter * 256 + 256)
+        acc = jnp.dot(t_ref[0, rows, :], qsc[0], preferred_element_type=F32)
+        for c in range(1, 8):
+            acc = acc + jnp.dot(t_ref[c, rows, :], qsc[c], preferred_element_type=F32)
+        for j in (1, 0):
+            k = SLOT[quarter * 2 + j]
             part = acc[j * ROWS : (j + 1) * ROWS]
             if k == 0:
                 w_own[...] = part
             else:
                 wb[k] = part.astype(BF16)
-                w_flight.append(send(wb.at[k], wr.at[k], w_send.at[k], w_recv.at[k], core, b_chip[k]))
+                w_flight[k].start()
+
+    for quarter in (3, 2, 1, 0):
+        w_chunk(quarter)
+        if quarter == 3:
+            loss_rows()
 
     mine = lax.broadcasted_iota(jnp.int32, total.shape, 0) == c_me
     s_row = jnp.sum(jnp.where(mine, total, 0.0), axis=0, keepdims=True)
@@ -265,14 +314,6 @@
     q_pull = (jnp.transpose(u_sum / s_row) - vbuf[0].astype(F32)) * INV_TEMP
     qs_ref[...] = slope(q_pull, q_unit[...], lens[0])
 
-    for copy in w_flight:
-        copy.wait_recv()
-    w_sum = w_own[...]
-    for k in range(1, 8):
-        w_sum = w_sum + wr[k].astype(F32)
-    v_pull = (w_sum - qbuf[c_me, pl.ds(lo, ROWS), :].astype(F32)) * INV_TEMP
-    cs_ref[...] = slope(v_pull, v_unit[...], lens[1])
-
     for copy in x_flight:
         copy.wait_recv()
     x_sum = xbuf[0]
@@ -280,8 +321,16 @@
         x_sum = x_sum + xbuf[b]
     hits_ref[...] = x_sum
 
-    for copy in copies:
+    for copy in copies + list(w_flight.values()):
         copy.wait_send()
+
+    for k in range(1, 8):
+        w_flight[k].wait_recv()
+    w_sum = w_own[...]
+    for k in range(1, 8):
+        w_sum = w_sum + wr[k].astype(F32)
+    v_pull = (w_sum - qbuf[c_me, pl.ds(lo, ROWS), :].astype(F32)) * INV_TEMP
+    cs_ref[...] = slope(v_pull, v_unit[...], lens[1])
 
 
 def write_out(l_ref, q_ref, v_ref, l_out, q_out, v_out, l_own, sem):
@@ -302,7 +351,7 @@
     vmem = pltpu.VMEM
     parts = pl.pallas_call(
         kernel,
-        out_shape=(vmem((8, ROWS), F32), vmem((ROWS, D), F32), vmem((ROWS, D), F32)),
+        out_shape=(vmem((1, ROWS), F32), vmem((ROWS, D), F32), vmem((ROWS, D), F32)),
         in_specs=[pl.BlockSpec(memory_space=pltpu.HBM)] * 2,
         out_specs=(pl.BlockSpec(memory_space=vmem),) * 3,
         scratch_shapes=[
@@ -315,6 +364,7 @@
             vmem((8, ROWS, D), BF16),
             vmem((8, 8 * ROWS, 2 * ROWS), BF16),
             vmem((16, 8, 2 * ROWS), F32),
+            vmem((2, 8, 8, 2 * ROWS), F32),
             vmem((2, 8, D, ROWS), BF16),
             vmem((8, D, ROWS), BF16),
             vmem((8, D, ROWS), BF16),
@@ -323,8 +373,8 @@
             vmem((8, ROWS, D), BF16),
             vmem((ROWS, D), F32),
             vmem((8, ROWS, D), BF16),
-            vmem((8, 8, ROWS), F32),
-            vmem((16, 8, ROWS), F32),
+            vmem((8, 1, ROWS), F32),
+            vmem((16, 1, ROWS), F32),
             dma((2,)),
             dma((8,)),
             dma((8,)),
@@ -345,6 +395,7 @@
             dma((16,)),
             pltpu.SemaphoreType.REGULAR((6,)),
             pltpu.SemaphoreType.REGULAR((2,)),
+            pltpu.SemaphoreType.REGULAR,
         ],
         compiler_params=pltpu.CompilerParams(collective_id=0, has_side_effects=True),
     )(queries, items)

time: 37.2 us -> 35.7 us (0.960)
  Pallas kernels: 36.4 us -> 34.5 us
    pallas_call x1, Pallas kernels: 35.6 us -> 33.8 us  [per_device(): pl.pallas_call(kernel, out_shape=(vmem((1, ROWS), F32), vmem((ROWS, D), F...]
where the time goes in v3:
time: 35.7 us; the launch traced here: 35.2 us
  Pallas kernels  34.5 us (97%)
  between operations  0.64 us (2%)
    pallas_call x1, Pallas kernels, per_device(): pl.pallas_call(kernel, out_shape=(vmem((1, ROWS), F32), vmem((ROWS, D), F...  33.8 us
    pallas_call x1, Pallas kernels, per_device(): pl.pallas_call(write_out, out_shape=(jax.ShapeDtypeStruct((1, 1), F32), j...  0.73 us

profile of v3, /device:TPU:1, one launch (start us, length us, event | category | flops | bytes accessed | tf_op | source)
XLA Modules:
  0.0 35.2 jit_solution(4437446850636192886)
XLA Ops:
  0.6 33.8 %shard_map.49 = (f32[1,128]{1,0:T(1,128)S(1)}, f32[128,256]{1,0:T(8,128)S(1)}, f32[128,256]{1,0:T(8,128)S(1)}) custom-call(bf16[128,256]{1,0:T(8,128)(2,1)} %q_hbm.1, bf16[128,256]{1,0:T(8,128)(2,1)} %v_hbm.1), custom_call_target="tpu_custom_call" | custom-call | tf_op jit(solution)/shard_map/pallas_call | solution.py:352
  34.5 0.7 %shard_map.50 = (f32[1,1]{1,0:T(1,128)}, f32[128,256]{1,0:T(8,128)}, f32[128,256]{1,0:T(8,128)}) custom-call(f32[1,128]{1,0:T(1,128)S(1)} %get-tuple-element.9.l_ref, f32[128,256]{1,0:T(8,128)S(1)} %get-tuple-element.10.q_ref, f32[128,256]{1,0:T(8,128)S(1)} %get-tuple-element.11.v_ref), custom_call_target="tpu_custom_call" | custom-call | tf_op jit(solution)/shard_map/pallas_call | solution.py:402

commit v4 on v3

--- a/solution.py
+++ b/solution.py
@@ -16,6 +16,7 @@
 A_LOW = (True, True, True)
 SLOT = (0, 1, 2, 4, 3, 5, 6, 7)
 NEAR, FAR = (0, 1, 2, 4), (3, 5, 6, 7)
+V_WAVE = (None, 0, 0, 1, 0, 1, 1, 2)
 ORDER = (7, 3, 5, 6, 1, 2, 4)
 
 
@@ -55,7 +56,6 @@
     ud,
     us,
     ur,
-    qsc,
     wb,
     w_own,
     wr,
@@ -70,7 +70,8 @@
     v_recv,
     s_send,
     s_recv,
-    d_sem,
+    d_send,
+    d_recv,
     u_send,
     u_recv,
     w_send,
@@ -110,18 +111,16 @@
     b_me = rank(place, False)
     lo = pl.multiple_of(core * ROWS, ROWS)
 
-    copies = []
-
     def plan(src, dst, ssem, rsem, blk, chip):
         return pltpu.make_async_remote_copy(
             src_ref=src, dst_ref=dst, send_sem=ssem, recv_sem=rsem, device_id=(blk, chip), device_id_type=MESH
         )
 
     def send(*where):
-        copy = plan(*where)
-        copy.start()
-        copies.append(copy)
-        return copy
+        plan(*where).start()
+
+    def drain(ref, sem):
+        pltpu.make_async_copy(ref, ref, sem).wait()
 
     barrier = pltpu.get_barrier_semaphore()
 
@@ -160,28 +159,24 @@
 
     pl.semaphore_wait(barrier, 7)
     for d in range(3):
-        tell(near_sem.at[d], core, a_chip[1 << d][0])
-        tell(near_sem.at[3 + d], core, b_chip[1 << d])
-
-    q_flight, v_flight, f_flight = {}, {}, {}
+        tell(near_sem.at[0], core, a_chip[1 << d][0])
+        tell(near_sem.at[1], core, b_chip[1 << d])
 
     def gather_q(k):
-        q_flight[k] = send(q_own, q_own, q_send.at[k], q_recv.at[k], core, a_chip[k][0])
+        send(q_own, q_own, q_send, q_recv.at[k - 1], core, a_chip[k][0])
 
     def gather_v(k):
-        v_flight[k] = send(vbuf.at[0], vbuf.at[SLOT[k]], v_send.at[k], v_recv.at[k], core, b_chip[k])
-
-    f_flight[0] = send(q_own, q_own, f_send.at[0], f_recv.at[0], other, dp)
+        send(vbuf.at[0], vbuf.at[SLOT[k]], v_send, v_recv.at[V_WAVE[k]], core, b_chip[k])
+
+    send(q_own, q_own, f_send, f_recv.at[0], other, dp)
     for k in (1, 2, 4):
         gather_v(k)
         gather_q(k)
-    for d in range(3):
-        pl.semaphore_wait(near_sem.at[d], 1)
+    pl.semaphore_wait(near_sem.at[0], 3)
     tell(far_sem.at[0], core, a_chip[1][0])
     for k in (3, 5, 6):
         gather_q(k)
-    for d in range(3, 6):
-        pl.semaphore_wait(near_sem.at[d], 1)
+    pl.semaphore_wait(near_sem.at[1], 3)
     tell(far_sem.at[1], core, b_chip[1])
     for k in (3, 5, 6):
         gather_v(k)
@@ -191,99 +186,84 @@
     gather_v(7)
     tell(side_sem, other, dp)
     pl.semaphore_wait(side_sem, 1)
-    f_flight[7] = send(q_own, q_own, f_send.at[7], f_recv.at[7], other, a_chip[7][0])
+    send(q_own, q_own, f_send, f_recv.at[1], other, a_chip[7][0])
 
     def pass_on(ks):
         for k in ks:
             theirs = qbuf.at[a_chip[k][1], pl.ds(lo, ROWS)]
-            q_flight[k].wait_recv()
-            f_flight[k] = send(theirs, theirs, f_send.at[k], f_recv.at[k], other, dp)
-
-    def weigh(half, ks):
-        rows = slice(half * 512, half * 512 + 512)
-        v_half = vbuf[half * 4 : half * 4 + 4].reshape(512, D)
+            drain(theirs, q_recv.at[k - 1])
+            send(theirs, theirs, f_send, f_recv.at[0 if k in NEAR else 1], other, dp)
+
+    def weigh(part, first, last, ks):
+        rows = slice(first * ROWS, last * ROWS)
+        v_part = vbuf[first:last].reshape((last - first) * ROWS, D)
         for k in ks:
             c = a_chip[k][1]
-            logits = lax.dot_general(v_half, qbuf[c], (((1,), (1,)), ((), ())), preferred_element_type=F32)
+            logits = lax.dot_general(v_part, qbuf[c], (((1,), (1,)), ((), ())), preferred_element_type=F32)
             e = jnp.exp(logits * INV_TEMP)
-            spart[half, c, 0:1, :] = jnp.sum(e, axis=0, keepdims=True)
+            spart[part, c, 0:1, :] = jnp.sum(e, axis=0, keepdims=True)
             t_ref[c, rows, :] = e.astype(BF16)
 
     pass_on(NEAR[1:])
-    for k in NEAR[1:]:
-        v_flight[k].wait_recv()
-    for k in NEAR:
-        f_flight[k].wait_recv()
-    weigh(0, NEAR)
+    drain(vbuf.at[1:4], v_recv.at[0])
+    drain(qbuf.at[0:2], f_recv.at[0])
+    weigh(0, 0, 4, NEAR)
     pass_on(FAR[:3])
-    q_flight[7].wait_recv()
-    for k in FAR:
-        f_flight[k].wait_recv()
-    weigh(0, FAR)
-    for k in FAR:
-        v_flight[k].wait_recv()
-    weigh(1, range(8))
+    drain(vbuf.at[0], q_recv.at[6])
+    drain(qbuf.at[0:2], f_recv.at[1])
+    weigh(0, 0, 4, FAR)
+    drain(vbuf.at[4:7], v_recv.at[1])
+    weigh(1, 4, 7, range(8))
+    drain(vbuf.at[7], v_recv.at[2])
+    weigh(2, 7, 8, range(8))
     a_me = core * 8 + c_me
     for c in range(8):
-        sbuf[a_me, c : c + 1, :] = spart[0, c, 0:1, :] + spart[1, c, 0:1, :]
+        sbuf[a_me, c : c + 1, :] = spart[0, c, 0:1, :] + spart[1, c, 0:1, :] + spart[2, c, 0:1, :]
     v_all = vbuf[...].reshape(8 * ROWS, D)
 
     def exchange(ref, ssem, rsem):
-        flight = []
         for k in ORDER:
-            for i, blk in enumerate((core, other)):
-                n = 2 * k + i
-                flight.append(send(ref, ref, ssem.at[n], rsem.at[n], blk, a_chip[k][0]))
-        flight.append(send(ref, ref, ssem.at[0], rsem.at[0], other, dp))
-        return flight
-
-    s_flight = exchange(sbuf.at[a_me], s_send, s_recv)
-    y_flight = exchange(ybuf.at[a_me], y_send, y_recv)
+            for blk in (core, other):
+                send(ref, ref, ssem, rsem, blk, a_chip[k][0])
+        send(ref, ref, ssem, rsem, other, dp)
+
+    exchange(sbuf.at[a_me], s_send, s_recv)
+    exchange(ybuf.at[a_me], y_send, y_recv)
 
     for c in range(8):
         ut = lax.dot_general(v_all, t_ref[c], (((0,), (0,)), ((), ())), preferred_element_type=F32)
         ub[0, c] = ut[:, :ROWS].astype(BF16)
         ub[1, c] = ut[:, ROWS:].astype(BF16)
-    across = send(ub.at[other], ud, d_sem.at[0], d_sem.at[1], other, dp)
-
-    across.wait_recv()
+    send(ub.at[other], ud, d_send, d_recv, other, dp)
+
+    drain(ud, d_recv)
     for c in range(8):
         us[c] = (ub[core, c].astype(F32) + ud[c].astype(F32)).astype(BF16)
-    u_flight = [
-        send(us.at[a_chip[k][1]], ur.at[k], u_send.at[k], u_recv.at[k], core, a_chip[k][0]) for k in ORDER
-    ]
-
-    for copy in s_flight:
-        copy.wait_recv()
+    for k in ORDER:
+        send(us.at[a_chip[k][1]], ur.at[k], u_send, u_recv, core, a_chip[k][0])
+
+    drain(sbuf.at[0:15], s_recv)
     total = sbuf[0]
     for a in range(1, 16):
         total = total + sbuf[a]
-    inverse = jnp.transpose(1.0 / total)
-    for c in range(8):
-        qsc[c] = (qbuf[c].astype(F32) * inverse[:, c : c + 1]).astype(BF16)
-
-    x_flight = []
+    inverse = 1.0 / total
 
     def loss_rows():
-        for copy in y_flight:
-            copy.wait_recv()
+        drain(ybuf.at[0:15], y_recv)
         hits = ybuf[0]
         for a in range(1, 16):
             hits = hits + ybuf[a]
         logs = jnp.sum(jnp.log(total), axis=0, keepdims=True)
         xbuf[b_me] = (logs[:, :ROWS] + logs[:, ROWS:]) - hits * INV_TEMP
         for k in ORDER:
-            x_flight.append(send(xbuf.at[b_me], xbuf.at[b_me], x_send.at[k], x_recv.at[k], core, b_chip[k]))
-
-    w_flight = {
-        k: plan(wb.at[k], wr.at[k], w_send.at[k], w_recv.at[k], core, b_chip[k]) for k in range(1, 8)
-    }
+            send(xbuf.at[b_me], xbuf.at[b_me], x_send, x_recv, core, b_chip[k])
 
     def w_chunk(quarter):
         rows = slice(quarter * 256, quarter * 256 + 256)
-        acc = jnp.dot(t_ref[0, rows, :], qsc[0], preferred_element_type=F32)
-        for c in range(1, 8):
-            acc = acc + jnp.dot(t_ref[c, rows, :], qsc[c], preferred_element_type=F32)
+        acc = jnp.zeros((256, D), F32)
+        for c in range(8):
+            probs = (t_ref[c, rows, :].astype(F32) * inverse[c : c + 1, :]).astype(BF16)
+            acc = acc + jnp.dot(probs, qbuf[c], preferred_element_type=F32)
         for j in (1, 0):
             k = SLOT[quarter * 2 + j]
             part = acc[j * ROWS : (j + 1) * ROWS]
@@ -291,7 +271,7 @@
                 w_own[...] = part
             else:
                 wb[k] = part.astype(BF16)
-                w_flight[k].start()
+                send(wb.at[k], wr.at[k], w_send, w_recv, core, b_chip[k])
 
     for quarter in (3, 2, 1, 0):
         w_chunk(quarter)
@@ -306,26 +286,34 @@
         along = jnp.sum(unit * pull, axis=1, keepdims=True)
         return (pull - unit * along) / length
 
-    for copy in u_flight:
-        copy.wait_recv()
+    drain(ur.at[1:8], u_recv)
     u_sum = ub[core, c_me].astype(F32) + ud[c_me].astype(F32)
     for k in range(1, 8):
         u_sum = u_sum + ur[k].astype(F32)
     q_pull = (jnp.transpose(u_sum / s_row) - vbuf[0].astype(F32)) * INV_TEMP
     qs_ref[...] = slope(q_pull, q_unit[...], lens[0])
 
-    for copy in x_flight:
-        copy.wait_recv()
+    drain(xbuf.at[0:7], x_recv)
     x_sum = xbuf[0]
     for b in range(1, 8):
         x_sum = x_sum + xbuf[b]
     hits_ref[...] = x_sum
 
-    for copy in copies + list(w_flight.values()):
-        copy.wait_send()
-
-    for k in range(1, 8):
-        w_flight[k].wait_recv()
+    sent = (
+        (vbuf.at[0:7], q_send),
+        (qbuf.at[0:4], f_send),
+        (vbuf.at[0:7], v_send),
+        (sbuf.at[0:15], s_send),
+        (ybuf.at[0:15], y_send),
+        (ud, d_send),
+        (ur.at[1:8], u_send),
+        (xbuf.at[0:7], x_send),
+        (wr.at[1:8], w_send),
+    )
+    for ref, sem in sent:
+        drain(ref, sem)
+
+    drain(wr.at[1:8], w_recv)
     w_sum = w_own[...]
     for k in range(1, 8):
         w_sum = w_sum + wr[k].astype(F32)
@@ -364,36 +352,36 @@
             vmem((8, ROWS, D), BF16),
             vmem((8, 8 * ROWS, 2 * ROWS), BF16),
             vmem((16, 8, 2 * ROWS), F32),
-            vmem((2, 8, 8, 2 * ROWS), F32),
+            vmem((3, 8, 8, 2 * ROWS), F32),
             vmem((2, 8, D, ROWS), BF16),
             vmem((8, D, ROWS), BF16),
             vmem((8, D, ROWS), BF16),
             vmem((8, D, ROWS), BF16),
-            vmem((8, 2 * ROWS, D), BF16),
             vmem((8, ROWS, D), BF16),
             vmem((ROWS, D), F32),
             vmem((8, ROWS, D), BF16),
             vmem((8, 1, ROWS), F32),
             vmem((16, 1, ROWS), F32),
             dma((2,)),
-            dma((8,)),
-            dma((8,)),
-            dma((8,)),
-            dma((8,)),
-            dma((8,)),
-            dma((8,)),
-            dma((16,)),
-            dma((16,)),
+            dma,
+            dma((7,)),
+            dma,
             dma((2,)),
-            dma((8,)),
-            dma((8,)),
-            dma((8,)),
-            dma((8,)),
-            dma((8,)),
-            dma((8,)),
-            dma((16,)),
-            dma((16,)),
-            pltpu.SemaphoreType.REGULAR((6,)),
+            dma,
+            dma((3,)),
+            dma,
+            dma,
+            dma,
+            dma,
+            dma,
+            dma,
+            dma,
+            dma,
+            dma,
+            dma,
+            dma,
+            dma,
+            pltpu.SemaphoreType.REGULAR((2,)),
             pltpu.SemaphoreType.REGULAR((2,)),
             pltpu.SemaphoreType.REGULAR,
         ],

time: 35.7 us -> 34.2 us (0.958)
  Pallas kernels: 34.5 us -> 33.3 us
    pallas_call x1, Pallas kernels: 33.8 us -> 32.5 us  [per_device(): pl.pallas_call(kernel, out_shape=(vmem((1, ROWS), F32), vmem((ROWS, D), F...]
where the time goes in v4:
time: 34.2 us; the launch traced here: 33.9 us
  Pallas kernels  33.3 us (97%)
  between operations  0.64 us (2%)
    pallas_call x1, Pallas kernels, per_device(): pl.pallas_call(kernel, out_shape=(vmem((1, ROWS), F32), vmem((ROWS, D), F...  32.5 us
    pallas_call x1, Pallas kernels, per_device(): pl.pallas_call(write_out, out_shape=(jax.ShapeDtypeStruct((1, 1), F32), j...  0.73 us

profile of v4, /device:TPU:1, one launch (start us, length us, event | category | flops | bytes accessed | tf_op | source)
XLA Modules:
  0.0 33.9 jit_solution(10571836895872613029)
XLA Ops:
  0.6 32.5 %shard_map.49 = (f32[1,128]{1,0:T(1,128)S(1)}, f32[128,256]{1,0:T(8,128)S(1)}, f32[128,256]{1,0:T(8,128)S(1)}) custom-call(bf16[128,256]{1,0:T(8,128)(2,1)} %q_hbm.1, bf16[128,256]{1,0:T(8,128)(2,1)} %v_hbm.1), custom_call_target="tpu_custom_call" | custom-call | tf_op jit(solution)/shard_map/pallas_call | solution.py:340
  33.2 0.7 %shard_map.50 = (f32[1,1]{1,0:T(1,128)}, f32[128,256]{1,0:T(8,128)}, f32[128,256]{1,0:T(8,128)}) custom-call(f32[1,128]{1,0:T(1,128)S(1)} %get-tuple-element.9.l_ref, f32[128,256]{1,0:T(8,128)S(1)} %get-tuple-element.10.q_ref, f32[128,256]{1,0:T(8,128)S(1)} %get-tuple-element.11.v_ref), custom_call_target="tpu_custom_call" | custom-call | tf_op jit(solution)/shard_map/pallas_call | solution.py:390

commit v5 on v4

--- a/solution.py
+++ b/solution.py
@@ -16,7 +16,8 @@
 A_LOW = (True, True, True)
 SLOT = (0, 1, 2, 4, 3, 5, 6, 7)
 NEAR, FAR = (0, 1, 2, 4), (3, 5, 6, 7)
-V_WAVE = (None, 0, 0, 1, 0, 1, 1, 2)
+WAVE = (None, 0, 0, 1, 0, 1, 1, 2)
+W_ORDER = ((7, 6), (5, 3), (4, 2), (1, 0))
 ORDER = (7, 3, 5, 6, 1, 2, 4)
 
 
@@ -42,8 +43,7 @@
     hits_ref,
     qs_ref,
     cs_ref,
-    q_in,
-    v_in,
+    given,
     q_unit,
     v_unit,
     lens,
@@ -62,27 +62,20 @@
     xbuf,
     ybuf,
     in_sem,
-    q_send,
     q_recv,
-    f_send,
     f_recv,
-    v_send,
     v_recv,
+    big_send,
+    small_send,
     s_send,
     s_recv,
-    d_send,
     d_recv,
-    u_send,
     u_recv,
-    w_send,
     w_recv,
-    x_send,
     x_recv,
-    y_send,
     y_recv,
     near_sem,
     far_sem,
-    side_sem,
 ):
     core = lax.axis_index("blk")
     other = 1 - core
@@ -132,20 +125,17 @@
         tell(barrier, core, b_chip[1 << d])
     tell(barrier, other, dp)
 
-    load_q = pltpu.make_async_copy(q_hbm, q_in, in_sem.at[0])
-    load_v = pltpu.make_async_copy(v_hbm, v_in, in_sem.at[1])
-    load_q.start()
-    load_v.start()
-    load_q.wait()
-    load_v.wait()
+    pltpu.make_async_copy(q_hbm, given.at[0], in_sem).start()
+    pltpu.make_async_copy(v_hbm, given.at[1], in_sem).start()
+    drain(given, in_sem)
 
     def unit_rows(value):
         wide = value.astype(F32)
         length = jnp.sqrt(jnp.sum(wide * wide, axis=1, keepdims=True) + TINY)
         return wide / length, length
 
-    qu, ql = unit_rows(q_in[...])
-    vu, vl = unit_rows(v_in[...])
+    qu, ql = unit_rows(given[0])
+    vu, vl = unit_rows(given[1])
     q_hat, v_hat = qu.astype(BF16), vu.astype(BF16)
     q_unit[...] = qu
     v_unit[...] = vu
@@ -163,12 +153,12 @@
         tell(near_sem.at[1], core, b_chip[1 << d])
 
     def gather_q(k):
-        send(q_own, q_own, q_send, q_recv.at[k - 1], core, a_chip[k][0])
+        send(q_own, q_own, big_send, q_recv.at[WAVE[k]], core, a_chip[k][0])
 
     def gather_v(k):
-        send(vbuf.at[0], vbuf.at[SLOT[k]], v_send, v_recv.at[V_WAVE[k]], core, b_chip[k])
-
-    send(q_own, q_own, f_send, f_recv.at[0], other, dp)
+        send(vbuf.at[0], vbuf.at[SLOT[k]], big_send, v_recv.at[WAVE[k]], core, b_chip[k])
+
+    send(q_own, q_own, big_send, f_recv.at[0], other, dp)
     for k in (1, 2, 4):
         gather_v(k)
         gather_q(k)
@@ -184,15 +174,11 @@
     gather_q(7)
     pl.semaphore_wait(far_sem.at[1], 1)
     gather_v(7)
-    tell(side_sem, other, dp)
-    pl.semaphore_wait(side_sem, 1)
-    send(q_own, q_own, f_send, f_recv.at[1], other, a_chip[7][0])
-
     def pass_on(ks):
+        drain(vbuf.at[0 : len(ks)], q_recv.at[WAVE[ks[0]]])
         for k in ks:
             theirs = qbuf.at[a_chip[k][1], pl.ds(lo, ROWS)]
-            drain(theirs, q_recv.at[k - 1])
-            send(theirs, theirs, f_send, f_recv.at[0 if k in NEAR else 1], other, dp)
+            send(theirs, theirs, big_send, f_recv.at[0 if k in NEAR else 1], other, dp)
 
     def weigh(part, first, last, ks):
         rows = slice(first * ROWS, last * ROWS)
@@ -207,9 +193,9 @@
     pass_on(NEAR[1:])
     drain(vbuf.at[1:4], v_recv.at[0])
     drain(qbuf.at[0:2], f_recv.at[0])
+    pass_on(FAR[:3])
     weigh(0, 0, 4, NEAR)
-    pass_on(FAR[:3])
-    drain(vbuf.at[0], q_recv.at[6])
+    pass_on(FAR[3:])
     drain(qbuf.at[0:2], f_recv.at[1])
     weigh(0, 0, 4, FAR)
     drain(vbuf.at[4:7], v_recv.at[1])
@@ -228,25 +214,26 @@
         send(ref, ref, ssem, rsem, other, dp)
 
     exchange(sbuf.at[a_me], s_send, s_recv)
-    exchange(ybuf.at[a_me], y_send, y_recv)
+    exchange(ybuf.at[a_me], small_send, y_recv)
 
     for c in range(8):
         ut = lax.dot_general(v_all, t_ref[c], (((0,), (0,)), ((), ())), preferred_element_type=F32)
         ub[0, c] = ut[:, :ROWS].astype(BF16)
         ub[1, c] = ut[:, ROWS:].astype(BF16)
-    send(ub.at[other], ud, d_send, d_recv, other, dp)
+    send(ub.at[other], ud, big_send, d_recv, other, dp)
 
     drain(ud, d_recv)
     for c in range(8):
         us[c] = (ub[core, c].astype(F32) + ud[c].astype(F32)).astype(BF16)
     for k in ORDER:
-        send(us.at[a_chip[k][1]], ur.at[k], u_send, u_recv, core, a_chip[k][0])
+        send(us.at[a_chip[k][1]], ur.at[k], big_send, u_recv, core, a_chip[k][0])
 
     drain(sbuf.at[0:15], s_recv)
     total = sbuf[0]
     for a in range(1, 16):
         total = total + sbuf[a]
     inverse = 1.0 / total
+    scales = [jnp.broadcast_to(inverse[c : c + 1, :], (1, 16, 2 * ROWS)).astype(BF16) for c in range(8)]
 
     def loss_rows():
         drain(ybuf.at[0:15], y_recv)
@@ -256,26 +243,24 @@
         logs = jnp.sum(jnp.log(total), axis=0, keepdims=True)
         xbuf[b_me] = (logs[:, :ROWS] + logs[:, ROWS:]) - hits * INV_TEMP
         for k in ORDER:
-            send(xbuf.at[b_me], xbuf.at[b_me], x_send, x_recv, core, b_chip[k])
-
-    def w_chunk(quarter):
-        rows = slice(quarter * 256, quarter * 256 + 256)
-        acc = jnp.zeros((256, D), F32)
+            send(xbuf.at[b_me], xbuf.at[b_me], small_send, x_recv, core, b_chip[k])
+
+    def pull_items(ks):
+        acc = jnp.zeros((2 * ROWS, D), F32)
         for c in range(8):
-            probs = (t_ref[c, rows, :].astype(F32) * inverse[c : c + 1, :]).astype(BF16)
-            acc = acc + jnp.dot(probs, qbuf[c], preferred_element_type=F32)
-        for j in (1, 0):
-            k = SLOT[quarter * 2 + j]
-            part = acc[j * ROWS : (j + 1) * ROWS]
+            rows = [t_ref[c, SLOT[k] * ROWS : (SLOT[k] + 1) * ROWS, :] for k in ks]
+            probs = jnp.concatenate(rows).reshape(16, 16, 2 * ROWS) * scales[c]
+            acc = acc + jnp.dot(probs.reshape(2 * ROWS, 2 * ROWS), qbuf[c], preferred_element_type=F32)
+        for k, part in zip(ks, (acc[:ROWS], acc[ROWS:])):
             if k == 0:
                 w_own[...] = part
             else:
                 wb[k] = part.astype(BF16)
-                send(wb.at[k], wr.at[k], w_send, w_recv, core, b_chip[k])
-
-    for quarter in (3, 2, 1, 0):
-        w_chunk(quarter)
-        if quarter == 3:
+                send(wb.at[k], wr.at[k], big_send, w_recv, core, b_chip[k])
+
+    for n, ks in enumerate(W_ORDER):
+        pull_items(ks)
+        if n == 0:
             loss_rows()
 
     mine = lax.broadcasted_iota(jnp.int32, total.shape, 0) == c_me
@@ -299,19 +284,9 @@
         x_sum = x_sum + xbuf[b]
     hits_ref[...] = x_sum
 
-    sent = (
-        (vbuf.at[0:7], q_send),
-        (qbuf.at[0:4], f_send),
-        (vbuf.at[0:7], v_send),
-        (sbuf.at[0:15], s_send),
-        (ybuf.at[0:15], y_send),
-        (ud, d_send),
-        (ur.at[1:8], u_send),
-        (xbuf.at[0:7], x_send),
-        (wr.at[1:8], w_send),
-    )
-    for ref, sem in sent:
-        drain(ref, sem)
+    drain(t_ref.at[:, 0:704, :], big_send)
+    drain(sbuf.at[0:15], s_send)
+    drain(ybuf.at[0:22], small_send)
 
     drain(wr.at[1:8], w_recv)
     w_sum = w_own[...]
@@ -343,8 +318,7 @@
         in_specs=[pl.BlockSpec(memory_space=pltpu.HBM)] * 2,
         out_specs=(pl.BlockSpec(memory_space=vmem),) * 3,
         scratch_shapes=[
-            vmem((ROWS, D), BF16),
-            vmem((ROWS, D), BF16),
+            vmem((2, ROWS, D), BF16),
             vmem((ROWS, D), F32),
             vmem((ROWS, D), F32),
             vmem((2, ROWS, 1), F32),
@@ -361,17 +335,11 @@
             vmem((ROWS, D), F32),
             vmem((8, ROWS, D), BF16),
             vmem((8, 1, ROWS), F32),
-            vmem((16, 1, ROWS), F32),
+            vmem((24, 1, ROWS), F32),
+            dma,
+            dma((3,)),
             dma((2,)),
-            dma,
-            dma((7,)),
-            dma,
-            dma((2,)),
-            dma,
             dma((3,)),
-            dma,
-            dma,
-            dma,
             dma,
             dma,
             dma,
@@ -383,7 +351,6 @@
             dma,
             pltpu.SemaphoreType.REGULAR((2,)),
             pltpu.SemaphoreType.REGULAR((2,)),
-            pltpu.SemaphoreType.REGULAR,
         ],
         compiler_params=pltpu.CompilerParams(collective_id=0, has_side_effects=True),
     )(queries, items)

time: 34.2 us -> 33.8 us (0.988)
  no operation moved by 1% of the time
where the time goes in v5:
time: 33.8 us; the launch traced here: 33.6 us
  Pallas kernels  33 us (98%)
  between operations  0.64 us (2%)
    pallas_call x1, Pallas kernels, per_device(): pl.pallas_call(kernel, out_shape=(vmem((1, ROWS), F32), vmem((ROWS, D), F...  32.2 us
    pallas_call x1, Pallas kernels, per_device(): pl.pallas_call(write_out, out_shape=(jax.ShapeDtypeStruct((1, 1), F32), j...  0.73 us

profile of v5, /device:TPU:1, one launch (start us, length us, event | category | flops | bytes accessed | tf_op | source)
XLA Modules:
  0.0 33.6 jit_solution(3930879737482265664)
XLA Ops:
  0.6 32.2 %shard_map.49 = (f32[1,128]{1,0:T(1,128)S(1)}, f32[128,256]{1,0:T(8,128)S(1)}, f32[128,256]{1,0:T(8,128)S(1)}) custom-call(bf16[128,256]{1,0:T(8,128)(2,1)} %q_hbm.1, bf16[128,256]{1,0:T(8,128)(2,1)} %v_hbm.1), custom_call_target="tpu_custom_call" | custom-call | tf_op jit(solution)/shard_map/pallas_call | solution.py:315
  32.9 0.7 %shard_map.50 = (f32[1,1]{1,0:T(1,128)}, f32[128,256]{1,0:T(8,128)}, f32[128,256]{1,0:T(8,128)}) custom-call(f32[1,128]{1,0:T(1,128)S(1)} %get-tuple-element.9.l_ref, f32[128,256]{1,0:T(8,128)S(1)} %get-tuple-element.10.q_ref, f32[128,256]{1,0:T(8,128)S(1)} %get-tuple-element.11.v_ref), custom_call_target="tpu_custom_call" | custom-call | tf_op jit(solution)/shard_map/pallas_call | solution.py:357

commit v6 on v5

--- a/solution.py
+++ b/solution.py
@@ -1,3 +1,5 @@
+import functools
+
 import jax
 import jax.numpy as jnp
 from jax import lax
@@ -13,11 +15,11 @@
 TINY = 1e-12
 F32 = jnp.float32
 BF16 = jnp.bfloat16
-A_LOW = (True, True, True)
+A_LOW = (True, False, True)
 SLOT = (0, 1, 2, 4, 3, 5, 6, 7)
 NEAR, FAR = (0, 1, 2, 4), (3, 5, 6, 7)
 WAVE = (None, 0, 0, 1, 0, 1, 1, 2)
-W_ORDER = ((7, 6), (5, 3), (4, 2), (1, 0))
+W_ORDER = ((0,), (2, 1), (3, 4), (6, 5), (7,))
 ORDER = (7, 3, 5, 6, 1, 2, 4)
 
 
@@ -102,6 +104,8 @@
     b_chip = [number(partner(k, False)) for k in range(8)]
     c_me = a_chip[0][1]
     b_me = rank(place, False)
+
+    b_bits = [high_bit(p) if is_low else low_bit(p) for p, is_low in zip(place, A_LOW)]
     lo = pl.multiple_of(core * ROWS, ROWS)
 
     def plan(src, dst, ssem, rsem, blk, chip):
@@ -245,21 +249,42 @@
         for k in ORDER:
             send(xbuf.at[b_me], xbuf.at[b_me], small_send, x_recv, core, b_chip[k])
 
-    def pull_items(ks):
-        acc = jnp.zeros((2 * ROWS, D), F32)
+    def pull(rows, n):
+        acc = jnp.zeros((n, D), F32)
         for c in range(8):
-            rows = [t_ref[c, SLOT[k] * ROWS : (SLOT[k] + 1) * ROWS, :] for k in ks]
-            probs = jnp.concatenate(rows).reshape(16, 16, 2 * ROWS) * scales[c]
-            acc = acc + jnp.dot(probs.reshape(2 * ROWS, 2 * ROWS), qbuf[c], preferred_element_type=F32)
-        for k, part in zip(ks, (acc[:ROWS], acc[ROWS:])):
-            if k == 0:
-                w_own[...] = part
-            else:
-                wb[k] = part.astype(BF16)
-                send(wb.at[k], wr.at[k], big_send, w_recv, core, b_chip[k])
-
-    for n, ks in enumerate(W_ORDER):
-        pull_items(ks)
+            probs = rows(c).reshape(n // 16, 16, 2 * ROWS) * scales[c]
+            acc = acc + jnp.dot(probs.reshape(n, 2 * ROWS), qbuf[c], preferred_element_type=F32)
+        return acc
+
+    def give(k, part, chip):
+        wb[k] = part.astype(BF16)
+        send(wb.at[k], wr.at[k], big_send, w_recv, core, chip)
+
+    def keep(part):
+        w_own[...] = part
+
+    for n, targets in enumerate(W_ORDER):
+        ks, rows, chips = [], [], []
+        for b in targets:
+            bits = ((b >> 2) & 1, (b >> 1) & 1, b & 1)
+            dz, dy, dx = (1 - own if bit else own for bit, own in zip(bits, b_bits))
+            k = 4 * dz + 2 * dy + dx
+            slot = k - dz * (1 - dy) * (1 - dx) + (1 - dz) * dy * dx
+            ks.append(k)
+            rows.append(pl.ds(pl.multiple_of(slot * ROWS, ROWS), ROWS))
+            chips.append(
+                number(
+                    [
+                        (3 - low_bit(p) if bit else low_bit(p)) if is_low else high_bit(p) * (3 - 2 * bit) + bit
+                        for p, bit, is_low in zip(place, bits, A_LOW)
+                    ]
+                )
+            )
+        acc = pull(lambda c: jnp.concatenate([t_ref[c, r, :] for r in rows]), len(targets) * ROWS)
+        for m, b in enumerate(targets):
+            part = acc[m * ROWS : (m + 1) * ROWS]
+            pl.when(b_me == b)(functools.partial(keep, part))
+            pl.when(b_me != b)(functools.partial(give, ks[m], part, chips[m]))
         if n == 0:
             loss_rows()
 

time: 33.8 us -> 33.1 us (0.979)
  Pallas kernels: 33 us -> 32.3 us
    pallas_call x1, Pallas kernels: 32.2 us -> 31.6 us  [per_device(): pl.pallas_call(kernel, out_shape=(vmem((1, ROWS), F32), vmem((ROWS, D), F...]
where the time goes in v6:
time: 33.1 us; the launch traced here: 32.9 us
  Pallas kernels  32.3 us (98%)
  between operations  0.64 us (2%)
    pallas_call x1, Pallas kernels, per_device(): pl.pallas_call(kernel, out_shape=(vmem((1, ROWS), F32), vmem((ROWS, D), F...  31.6 us
    pallas_call x1, Pallas kernels, per_device(): pl.pallas_call(write_out, out_shape=(jax.ShapeDtypeStruct((1, 1), F32), j...  0.73 us

profile of v6, /device:TPU:1, one launch (start us, length us, event | category | flops | bytes accessed | tf_op | source)
XLA Modules:
  0.0 32.9 jit_solution(10655080769654942761)
XLA Ops:
  0.6 31.6 %shard_map.49 = (f32[1,128]{1,0:T(1,128)S(1)}, f32[128,256]{1,0:T(8,128)S(1)}, f32[128,256]{1,0:T(8,128)S(1)}) custom-call(bf16[128,256]{1,0:T(8,128)(2,1)} %q_hbm.1, bf16[128,256]{1,0:T(8,128)(2,1)} %v_hbm.1), custom_call_target="tpu_custom_call" | custom-call | tf_op jit(solution)/shard_map/pallas_call | solution.py:340
  32.2 0.7 %shard_map.50 = (f32[1,1]{1,0:T(1,128)}, f32[128,256]{1,0:T(8,128)}, f32[128,256]{1,0:T(8,128)}) custom-call(f32[1,128]{1,0:T(1,128)S(1)} %get-tuple-element.9.l_ref, f32[128,256]{1,0:T(8,128)S(1)} %get-tuple-element.10.q_ref, f32[128,256]{1,0:T(8,128)S(1)} %get-tuple-element.11.v_ref), custom_call_target="tpu_custom_call" | custom-call | tf_op jit(solution)/shard_map/pallas_call | solution.py:382

commit v7 on v6

--- a/solution.py
+++ b/solution.py
@@ -24,7 +24,7 @@
 
 
 def flip_low(p, d):
-    return p + 1 - 2 * lax.rem(p, 2) if d else p
+    return p + 1 - 2 * (p & 1) if d else p
 
 
 def flip_high(p, d):
@@ -32,11 +32,11 @@
 
 
 def low_bit(p):
-    return lax.rem(lax.div(p + 1, 2), 2)
+    return ((p + 1) >> 1) & 1
 
 
 def high_bit(p):
-    return lax.div(p, 2)
+    return p >> 1
 
 
 def kernel(
@@ -82,7 +82,7 @@
     core = lax.axis_index("blk")
     other = 1 - core
     dp = lax.axis_index("dp")
-    z, y, x = lax.div(dp, 16), lax.rem(lax.div(dp, 4), 4), lax.rem(dp, 4)
+    z, y, x = dp >> 4, (dp >> 2) & 3, dp & 3
 
     place = (z, y, x)
 
@@ -100,6 +100,21 @@
     def number(place):
         return place[0] * 16 + place[1] * 4 + place[2]
 
+    a_place = {k: partner(k, True) for k in (1, 2, 4)}
+    b_place = {k: partner(k, False) for k in (1, 2, 4)}
+    barrier = pltpu.get_barrier_semaphore()
+
+    def tell(sem, blk, chip):
+        pl.semaphore_signal(sem, inc=1, device_id=(blk, chip), device_id_type=MESH)
+
+    tell(barrier, other, dp)
+    for k in (1, 2, 4):
+        tell(barrier, core, number(b_place[k]))
+        tell(barrier, core, number(a_place[k]))
+
+    pltpu.make_async_copy(q_hbm, given.at[0], in_sem).start()
+    pltpu.make_async_copy(v_hbm, given.at[1], in_sem).start()
+
     a_chip = [(number(partner(k, True)), rank(partner(k, True), True)) for k in range(8)]
     b_chip = [number(partner(k, False)) for k in range(8)]
     c_me = a_chip[0][1]
@@ -119,18 +134,6 @@
     def drain(ref, sem):
         pltpu.make_async_copy(ref, ref, sem).wait()
 
-    barrier = pltpu.get_barrier_semaphore()
-
-    def tell(sem, blk, chip):
-        pl.semaphore_signal(sem, inc=1, device_id=(blk, chip), device_id_type=MESH)
-
-    for d in range(3):
-        tell(barrier, core, a_chip[1 << d][0])
-        tell(barrier, core, b_chip[1 << d])
-    tell(barrier, other, dp)
-
-    pltpu.make_async_copy(q_hbm, given.at[0], in_sem).start()
-    pltpu.make_async_copy(v_hbm, given.at[1], in_sem).start()
     drain(given, in_sem)
 
     def unit_rows(value):

time: 33.1 us -> 32.8 us (level)
  no operation moved by 1% of the time
where the time goes in v7:
time: 32.8 us; the launch traced here: 32.7 us
  Pallas kernels  32 us (98%)
  between operations  0.64 us (2%)
    pallas_call x1, Pallas kernels, per_device(): pl.pallas_call(kernel, out_shape=(vmem((1, ROWS), F32), vmem((ROWS, D), F...  31.3 us
    pallas_call x1, Pallas kernels, per_device(): pl.pallas_call(write_out, out_shape=(jax.ShapeDtypeStruct((1, 1), F32), j...  0.73 us

profile of v7, /device:TPU:1, one launch (start us, length us, event | category | flops | bytes accessed | tf_op | source)
XLA Modules:
  0.0 32.7 jit_solution(15886768162301432296)
XLA Ops:
  0.6 31.3 %shard_map.49 = (f32[1,128]{1,0:T(1,128)S(1)}, f32[128,256]{1,0:T(8,128)S(1)}, f32[128,256]{1,0:T(8,128)S(1)}) custom-call(bf16[128,256]{1,0:T(8,128)(2,1)} %q_hbm.1, bf16[128,256]{1,0:T(8,128)(2,1)} %v_hbm.1), custom_call_target="tpu_custom_call" | custom-call | tf_op jit(solution)/shard_map/pallas_call | solution.py:343
  32.0 0.7 %shard_map.50 = (f32[1,1]{1,0:T(1,128)}, f32[128,256]{1,0:T(8,128)}, f32[128,256]{1,0:T(8,128)}) custom-call(f32[1,128]{1,0:T(1,128)S(1)} %get-tuple-element.9.l_ref, f32[128,256]{1,0:T(8,128)S(1)} %get-tuple-element.10.q_ref, f32[128,256]{1,0:T(8,128)S(1)} %get-tuple-element.11.v_ref), custom_call_target="tpu_custom_call" | custom-call | tf_op jit(solution)/shard_map/pallas_call | solution.py:385

commit v8 on v7

--- a/solution.py
+++ b/solution.py
@@ -12,6 +12,7 @@
 D = 256
 BATCH = 16384
 INV_TEMP = 20.0
+LOG2_E = 1.4426950408889634
 TINY = 1e-12
 F32 = jnp.float32
 BF16 = jnp.bfloat16
@@ -19,7 +20,7 @@
 SLOT = (0, 1, 2, 4, 3, 5, 6, 7)
 NEAR, FAR = (0, 1, 2, 4), (3, 5, 6, 7)
 WAVE = (None, 0, 0, 1, 0, 1, 1, 2)
-W_ORDER = ((0,), (2, 1), (3, 4), (6, 5), (7,))
+W_ORDER = ((0,), (2, 1), (4, 3), (6, 7), (5,))
 ORDER = (7, 3, 5, 6, 1, 2, 4)
 
 
@@ -193,7 +194,7 @@
         for k in ks:
             c = a_chip[k][1]
             logits = lax.dot_general(v_part, qbuf[c], (((1,), (1,)), ((), ())), preferred_element_type=F32)
-            e = jnp.exp(logits * INV_TEMP)
+            e = jnp.exp2(logits * (INV_TEMP * LOG2_E))
             spart[part, c, 0:1, :] = jnp.sum(e, axis=0, keepdims=True)
             t_ref[c, rows, :] = e.astype(BF16)
 

time: 32.8 us -> 32.6 us (level)
  no operation moved by 1% of the time
where the time goes in v8:
time: 32.6 us; the launch traced here: 32.4 us
  Pallas kernels  31.8 us (98%)
  between operations  0.64 us (2%)
    pallas_call x1, Pallas kernels, per_device(): pl.pallas_call(kernel, out_shape=(vmem((1, ROWS), F32), vmem((ROWS, D), F...  31.1 us
    pallas_call x1, Pallas kernels, per_device(): pl.pallas_call(write_out, out_shape=(jax.ShapeDtypeStruct((1, 1), F32), j...  0.73 us

profile of v8, /device:TPU:1, one launch (start us, length us, event | category | flops | bytes accessed | tf_op | source)
XLA Modules:
  0.0 32.4 jit_solution(14514131417572118124)
XLA Ops:
  0.6 31.1 %shard_map.49 = (f32[1,128]{1,0:T(1,128)S(1)}, f32[128,256]{1,0:T(8,128)S(1)}, f32[128,256]{1,0:T(8,128)S(1)}) custom-call(bf16[128,256]{1,0:T(8,128)(2,1)} %q_hbm.1, bf16[128,256]{1,0:T(8,128)(2,1)} %v_hbm.1), custom_call_target="tpu_custom_call" | custom-call | tf_op jit(solution)/shard_map/pallas_call | solution.py:344
  31.7 0.7 %shard_map.50 = (f32[1,1]{1,0:T(1,128)}, f32[128,256]{1,0:T(8,128)}, f32[128,256]{1,0:T(8,128)}) custom-call(f32[1,128]{1,0:T(1,128)S(1)} %get-tuple-element.9.l_ref, f32[128,256]{1,0:T(8,128)S(1)} %get-tuple-element.10.q_ref, f32[128,256]{1,0:T(8,128)S(1)} %get-tuple-element.11.v_ref), custom_call_target="tpu_custom_call" | custom-call | tf_op jit(solution)/shard_map/pallas_call | solution.py:386

commit v9 on v8

--- a/solution.py
+++ b/solution.py
@@ -167,16 +167,16 @@
         send(vbuf.at[0], vbuf.at[SLOT[k]], big_send, v_recv.at[WAVE[k]], core, b_chip[k])
 
     send(q_own, q_own, big_send, f_recv.at[0], other, dp)
-    for k in (1, 2, 4):
+    for k in (4, 2, 1):
         gather_v(k)
         gather_q(k)
     pl.semaphore_wait(near_sem.at[0], 3)
     tell(far_sem.at[0], core, a_chip[1][0])
-    for k in (3, 5, 6):
+    for k in (6, 5, 3):
         gather_q(k)
     pl.semaphore_wait(near_sem.at[1], 3)
     tell(far_sem.at[1], core, b_chip[1])
-    for k in (3, 5, 6):
+    for k in (6, 5, 3):
         gather_v(k)
     pl.semaphore_wait(far_sem.at[0], 1)
     gather_q(7)

time: 32.6 us -> 32.4 us (level)
  no operation moved by 1% of the time
where the time goes in v9:
time: 32.4 us; the launch traced here: 32.2 us
  Pallas kernels  31.6 us (98%)
  between operations  0.64 us (2%)
    pallas_call x1, Pallas kernels, per_device(): pl.pallas_call(kernel, out_shape=(vmem((1, ROWS), F32), vmem((ROWS, D), F...  30.8 us
    pallas_call x1, Pallas kernels, per_device(): pl.pallas_call(write_out, out_shape=(jax.ShapeDtypeStruct((1, 1), F32), j...  0.73 us

profile of v9, /device:TPU:1, one launch (start us, length us, event | category | flops | bytes accessed | tf_op | source)
XLA Modules:
  0.0 32.2 jit_solution(10894066013297964899)
XLA Ops:
  0.6 30.8 %shard_map.49 = (f32[1,128]{1,0:T(1,128)S(1)}, f32[128,256]{1,0:T(8,128)S(1)}, f32[128,256]{1,0:T(8,128)S(1)}) custom-call(bf16[128,256]{1,0:T(8,128)(2,1)} %q_hbm.1, bf16[128,256]{1,0:T(8,128)(2,1)} %v_hbm.1), custom_call_target="tpu_custom_call" | custom-call | tf_op jit(solution)/shard_map/pallas_call | solution.py:344
  31.5 0.7 %shard_map.50 = (f32[1,1]{1,0:T(1,128)}, f32[128,256]{1,0:T(8,128)}, f32[128,256]{1,0:T(8,128)}) custom-call(f32[1,128]{1,0:T(1,128)S(1)} %get-tuple-element.9.l_ref, f32[128,256]{1,0:T(8,128)S(1)} %get-tuple-element.10.q_ref, f32[128,256]{1,0:T(8,128)S(1)} %get-tuple-element.11.v_ref), custom_call_target="tpu_custom_call" | custom-call | tf_op jit(solution)/shard_map/pallas_call | solution.py:386

commit v10 on v9

--- a/solution.py
+++ b/solution.py
@@ -16,11 +16,11 @@
 TINY = 1e-12
 F32 = jnp.float32
 BF16 = jnp.bfloat16
-A_LOW = (True, False, True)
+A_LOW = (True, True, True)
 SLOT = (0, 1, 2, 4, 3, 5, 6, 7)
 NEAR, FAR = (0, 1, 2, 4), (3, 5, 6, 7)
 WAVE = (None, 0, 0, 1, 0, 1, 1, 2)
-W_ORDER = ((0,), (2, 1), (4, 3), (6, 7), (5,))
+W_ORDER = ((0,), (1, 2), (4, 3), (5, 6), (7,))
 ORDER = (7, 3, 5, 6, 1, 2, 4)
 
 

time: 32.4 us -> 31.4 us (0.969)
  Pallas kernels: 31.6 us -> 30.7 us
    pallas_call x1, Pallas kernels: 30.8 us -> 29.9 us  [per_device(): pl.pallas_call(kernel, out_shape=(vmem((1, ROWS), F32), vmem((ROWS, D), F...]
where the time goes in v10:
time: 31.4 us; the launch traced here: 31.3 us
  Pallas kernels  30.7 us (98%)
  between operations  0.64 us (2%)
    pallas_call x1, Pallas kernels, per_device(): pl.pallas_call(kernel, out_shape=(vmem((1, ROWS), F32), vmem((ROWS, D), F...  29.9 us
    pallas_call x1, Pallas kernels, per_device(): pl.pallas_call(write_out, out_shape=(jax.ShapeDtypeStruct((1, 1), F32), j...  0.73 us

profile of v10, /device:TPU:1, one launch (start us, length us, event | category | flops | bytes accessed | tf_op | source)
XLA Modules:
  0.0 31.3 jit_solution(2203163603322339648)
XLA Ops:
  0.6 29.9 %shard_map.49 = (f32[1,128]{1,0:T(1,128)S(1)}, f32[128,256]{1,0:T(8,128)S(1)}, f32[128,256]{1,0:T(8,128)S(1)}) custom-call(bf16[128,256]{1,0:T(8,128)(2,1)} %q_hbm.1, bf16[128,256]{1,0:T(8,128)(2,1)} %v_hbm.1), custom_call_target="tpu_custom_call" | custom-call | tf_op jit(solution)/shard_map/pallas_call | solution.py:344
  30.6 0.7 %shard_map.50 = (f32[1,1]{1,0:T(1,128)}, f32[128,256]{1,0:T(8,128)}, f32[128,256]{1,0:T(8,128)}) custom-call(f32[1,128]{1,0:T(1,128)S(1)} %get-tuple-element.9.l_ref, f32[128,256]{1,0:T(8,128)S(1)} %get-tuple-element.10.q_ref, f32[128,256]{1,0:T(8,128)S(1)} %get-tuple-element.11.v_ref), custom_call_target="tpu_custom_call" | custom-call | tf_op jit(solution)/shard_map/pallas_call | solution.py:386

commit v11 on v10

--- a/solution.py
+++ b/solution.py
@@ -171,11 +171,11 @@
         gather_v(k)
         gather_q(k)
     pl.semaphore_wait(near_sem.at[0], 3)
-    tell(far_sem.at[0], core, a_chip[1][0])
+    tell(far_sem.at[0], core, a_chip[4][0])
     for k in (6, 5, 3):
         gather_q(k)
     pl.semaphore_wait(near_sem.at[1], 3)
-    tell(far_sem.at[1], core, b_chip[1])
+    tell(far_sem.at[1], core, b_chip[4])
     for k in (6, 5, 3):
         gather_v(k)
     pl.semaphore_wait(far_sem.at[0], 1)
@@ -333,9 +333,9 @@
     l_own[0, 0] = jnp.sum(l_ref[...]) / BATCH
     l_copy = pltpu.make_async_copy(l_own, l_out, sem.at[2])
     l_copy.start()
-    l_copy.wait()
     q_copy.wait()
     v_copy.wait()
+    l_copy.wait()
 
 
 def per_device(queries, items):

time: 31.4 us -> 31.5 us (level)
  no operation moved by 1% of the time
where the time goes in v11:
time: 31.5 us; the launch traced here: 31.3 us
  Pallas kernels  30.7 us (97%)
  between operations  0.64 us (2%)
    pallas_call x1, Pallas kernels, per_device(): pl.pallas_call(kernel, out_shape=(vmem((1, ROWS), F32), vmem((ROWS, D), F...  29.9 us
    pallas_call x1, Pallas kernels, per_device(): pl.pallas_call(write_out, out_shape=(jax.ShapeDtypeStruct((1, 1), F32), j...  0.74 us

profile of v11, /device:TPU:1, one launch (start us, length us, event | category | flops | bytes accessed | tf_op | source)
XLA Modules:
  0.0 31.3 jit_solution(14209310863283024195)
XLA Ops:
  0.6 29.9 %shard_map.49 = (f32[1,128]{1,0:T(1,128)S(1)}, f32[128,256]{1,0:T(8,128)S(1)}, f32[128,256]{1,0:T(8,128)S(1)}) custom-call(bf16[128,256]{1,0:T(8,128)(2,1)} %q_hbm.1, bf16[128,256]{1,0:T(8,128)(2,1)} %v_hbm.1), custom_call_target="tpu_custom_call" | custom-call | tf_op jit(solution)/shard_map/pallas_call | solution.py:344
  30.6 0.7 %shard_map.50 = (f32[1,1]{1,0:T(1,128)}, f32[128,256]{1,0:T(8,128)}, f32[128,256]{1,0:T(8,128)}) custom-call(f32[1,128]{1,0:T(1,128)S(1)} %get-tuple-element.9.l_ref, f32[128,256]{1,0:T(8,128)S(1)} %get-tuple-element.10.q_ref, f32[128,256]{1,0:T(8,128)S(1)} %get-tuple-element.11.v_ref), custom_call_target="tpu_custom_call" | custom-call | tf_op jit(solution)/shard_map/pallas_call | solution.py:386

commit v12 on v10

--- a/solution.py
+++ b/solution.py
@@ -289,7 +289,7 @@
             part = acc[m * ROWS : (m + 1) * ROWS]
             pl.when(b_me == b)(functools.partial(keep, part))
             pl.when(b_me != b)(functools.partial(give, ks[m], part, chips[m]))
-        if n == 0:
+        if n == 1:
             loss_rows()
 
     mine = lax.broadcasted_iota(jnp.int32, total.shape, 0) == c_me

time: 31.4 us -> 32.6 us (1.038)
  Pallas kernels: 30.7 us -> 31.8 us
    pallas_call x1, Pallas kernels: 29.9 us -> 31.1 us  [per_device(): pl.pallas_call(kernel, out_shape=(vmem((1, ROWS), F32), vmem((ROWS, D), F...]
where the time goes in v12:
time: 32.6 us; the launch traced here: 32.5 us
  Pallas kernels  31.8 us (98%)
  between operations  0.64 us (2%)
    pallas_call x1, Pallas kernels, per_device(): pl.pallas_call(kernel, out_shape=(vmem((1, ROWS), F32), vmem((ROWS, D), F...  31.1 us
    pallas_call x1, Pallas kernels, per_device(): pl.pallas_call(write_out, out_shape=(jax.ShapeDtypeStruct((1, 1), F32), j...  0.73 us

profile of v12, /device:TPU:1, one launch (start us, length us, event | category | flops | bytes accessed | tf_op | source)
XLA Modules:
  0.0 32.5 jit_solution(1105224760243305894)
XLA Ops:
  0.6 31.1 %shard_map.49 = (f32[1,128]{1,0:T(1,128)S(1)}, f32[128,256]{1,0:T(8,128)S(1)}, f32[128,256]{1,0:T(8,128)S(1)}) custom-call(bf16[128,256]{1,0:T(8,128)(2,1)} %q_hbm.1, bf16[128,256]{1,0:T(8,128)(2,1)} %v_hbm.1), custom_call_target="tpu_custom_call" | custom-call | tf_op jit(solution)/shard_map/pallas_call | solution.py:344
  31.7 0.7 %shard_map.50 = (f32[1,1]{1,0:T(1,128)}, f32[128,256]{1,0:T(8,128)}, f32[128,256]{1,0:T(8,128)}) custom-call(f32[1,128]{1,0:T(1,128)S(1)} %get-tuple-element.9.l_ref, f32[128,256]{1,0:T(8,128)S(1)} %get-tuple-element.10.q_ref, f32[128,256]{1,0:T(8,128)S(1)} %get-tuple-element.11.v_ref), custom_call_target="tpu_custom_call" | custom-call | tf_op jit(solution)/shard_map/pallas_call | solution.py:386
